TPU v7x, 64 devices: a 2x2x8 block of a 4x4x8 slice. The times are simulated.
64 devices in a mesh: rep: 4 (over x, y), dp: 16 (over z, core).
Axes of the slice: x: 2, y: 2, z: 8, core: 2. Of those that a mesh axis runs over, the one named last changes fastest.
The devices are a block of a 4x4x8 slice.
Arguments:
- x: bfloat16 [64, 4096, 640], P(('rep', 'dp')), parts along dimension 0
- dy: bfloat16 [64, 4096, 640], P(('rep', 'dp')), parts along dimension 0
- w_gate: bfloat16 [2, 640, 1536], P(None, 'dp')
- w_up: bfloat16 [2, 640, 1536], P(None, 'dp')
- w_down: bfloat16 [2, 1536, 640], P(None, 'dp')
- m_w_gate: float32 [2, 640, 1536], P(None, 'dp')
- m_w_up: float32 [2, 640, 1536], P(None, 'dp')
- m_w_down: float32 [2, 1536, 640], P(None, 'dp')
- v_w_gate: float32 [2, 640, 1536], P(None, 'dp')
- v_w_up: float32 [2, 640, 1536], P(None, 'dp')
- v_w_down: float32 [2, 1536, 640], P(None, 'dp')
Outputs:
- output 1: bfloat16 [8, 640, 1536], P('rep', 'dp'), parts along dimension 0
- output 2: bfloat16 [8, 640, 1536], P('rep', 'dp'), parts along dimension 0
- output 3: bfloat16 [8, 1536, 640], P('rep', 'dp'), parts along dimension 0
- output 4: float32 [8, 640, 1536], P('rep', 'dp'), parts along dimension 0
- output 5: float32 [8, 640, 1536], P('rep', 'dp'), parts along dimension 0
- output 6: float32 [8, 1536, 640], P('rep', 'dp'), parts along dimension 0
- output 7: float32 [8, 640, 1536], P('rep', 'dp'), parts along dimension 0
- output 8: float32 [8, 640, 1536], P('rep', 'dp'), parts along dimension 0
- output 9: float32 [8, 1536, 640], P('rep', 'dp'), parts along dimension 0
There are 4 independent parts. A program takes and returns all parts, laid end to end along the dimension named above; an argument that names none is the same for every part.
All inputs are finite; a program needn't handle non-finite values.
Results may differ from a plain program's by a relative error of at most 0.0221.
Values are sent between devices in bfloat16 or wider.
A program may use at most 768 MiB of HBM per device.

v0:
```python
import functools

import jax
import jax.numpy as jnp
from jax import lax
from jax.experimental import pallas as pl
from jax.experimental.pallas import tpu as pltpu
from jax.sharding import PartitionSpec as P

MESH = pl.DeviceIdType.MESH
BF, F32 = jnp.bfloat16, jnp.float32
ANY = pl.BlockSpec(memory_space=pl.ANY)
VM = pl.BlockSpec(memory_space=pltpu.VMEM)
TILE = 512
COLS = 512
LIMIT = 60 * 1024 * 1024


def dot(a, b, ca=1, cb=0):
    return lax.dot_general(a, b, (((ca,), (cb,)), ((), ())), preferred_element_type=F32)


def rounded(a):
    return a.astype(BF).astype(F32)


def norm_of(h):
    wide = h.astype(F32)
    scale = lax.rsqrt(jnp.mean(wide * wide, -1, keepdims=True) + 1e-6)
    return wide, scale, (wide * scale).astype(BF)


def place():
    me = lax.axis_index("dp")
    z, c = me // 2, me % 2
    return z, c, lambda zz, cc: {"dp": zz * 2 + cc}


def greet(peers):
    barrier = pltpu.get_barrier_semaphore()
    for p in peers:
        pl.semaphore_signal(barrier, inc=1, device_id=p, device_id_type=MESH)
    pl.semaphore_wait(barrier, len(peers))


def reach(m, chips):
    far, near = chips // 2, chips - 1 - chips // 2
    return (far, near) if m % 2 == 0 else (near, far)


class Gather:
    def __init__(self, chips, m, src, out, sems):
        self.chips, self.m, self.src, self.out = chips, m, src, out
        self.ring_s, self.ring_r, self.side_s, self.side_r, self.own = sems
        self.rows = src.shape[0]
        self.z, self.c, self.dev = place()
        self.hops = reach(m, chips)
        self.sent = []

    def at(self, zz, cc):
        return self.out.at[pl.ds(pl.multiple_of((zz * 2 + cc) * self.rows, 8), self.rows)]

    def ring(self, way, k, src=None):
        step = 1 if way == 0 else -1
        origin = (self.z - step * k + self.chips) % self.chips
        to = (self.z + step + self.chips) % self.chips
        block = self.at(origin, self.c)
        i = (0 if way == 0 else self.hops[0]) + k
        return pltpu.make_async_remote_copy(
            src_ref=block if src is None else src, dst_ref=block, send_sem=self.ring_s.at[self.m, i], recv_sem=self.ring_r.at[self.m, i],
            device_id=self.dev(to, self.c), device_id_type=MESH)

    def side(self, origin, i, src=None):
        block = self.at(origin, self.c)
        return pltpu.make_async_remote_copy(
            src_ref=block if src is None else src, dst_ref=block, send_sem=self.side_s.at[self.m, i], recv_sem=self.side_r.at[self.m, i],
            device_id=self.dev(self.z, 1 - self.c), device_id_type=MESH)

    def start(self):
        for way in (0, 1):
            self.sent.append(self.ring(way, 0, self.src))
            self.sent[-1].start()
        self.sent.append(self.side(self.z, 0, self.src))
        self.sent[-1].start()
        self.local = pltpu.make_async_copy(self.src, self.at(self.z, self.c), self.own.at[self.m])
        self.local.start()

    def step(self, k):
        for way in (0, 1):
            if k > self.hops[way]:
                continue
            self.ring(way, k - 1).wait_recv()
            if k < self.hops[way]:
                self.sent.append(self.ring(way, k))
                self.sent[-1].start()
            origin = (self.z - (1 if way == 0 else -1) * k + self.chips) % self.chips
            self.sent.append(self.side(origin, k + (0 if way == 0 else self.hops[0])))
            self.sent[-1].start()

    def finish(self):
        for copy in self.sent:
            copy.wait_send()
        for i in range(self.chips):
            self.side(self.z, i).wait_recv()
        self.local.wait()


def gather_sems(n, chips):
    return [pltpu.SemaphoreType.DMA((n, chips - 1))] * 2 + [pltpu.SemaphoreType.DMA((n, chips))] * 2 + [pltpu.SemaphoreType.DMA((n,))]


def gather_kernel(chips, layers, *refs):
    shards, outs, sems = refs[:3], refs[3 : 3 + 3 * layers], refs[3 + 3 * layers :]
    z, c, dev = place()
    greet([dev((z + 1) % chips, c), dev((z + chips - 1) % chips, c), dev(z, 1 - c)])
    all_of = [Gather(chips, l * 3 + i, shards[i].at[l], outs[l * 3 + i], sems) for l in range(layers) for i in range(3)]
    for one in all_of:
        one.start()
    for k in range(1, chips // 2 + 1):
        for one in all_of:
            one.step(k)
    for one in all_of:
        one.finish()


def gather_all(weights, n):
    layers = weights[0].shape[0]
    chips = n // 2
    return pl.pallas_call(
        functools.partial(gather_kernel, chips, layers),
        out_shape=[jax.ShapeDtypeStruct((w.shape[1] * n, w.shape[2]), w.dtype) for _ in range(layers) for w in weights],
        in_specs=[VM] * 3,
        out_specs=[ANY] * (3 * layers),
        scratch_shapes=gather_sems(3 * layers, chips),
        compiler_params=pltpu.CompilerParams(collective_id=0, has_side_effects=True),
        name="gather",
    )(*weights)


class Scatter:
    def __init__(self, chips, l, grads, own, side, slots, sems):
        self.chips, self.l, self.grads, self.own, self.sides, self.slots = chips, l, grads, own, side, slots
        self.own_sem, self.side_s, self.side_r, self.ring_s, self.ring_r = sems
        self.z, self.c, self.dev = place()
        self.sent = []

    def part(self, i, zz, cc):
        rows = self.own[i].shape[-2]
        return self.grads[i].at[pl.ds(pl.multiple_of((zz * 2 + cc) * rows, 8), rows)]

    def chunk(self, way, k):
        return (self.z - 1 - k + 2 * self.chips) % self.chips if way == 0 else (self.z + 1 + k) % self.chips

    def local(self, i, zz):
        return pltpu.make_async_copy(self.part(i, zz, self.c), self.own[i].at[self.l, zz], self.own_sem.at[self.l, i, zz])

    def side(self, i, zz):
        return pltpu.make_async_remote_copy(
            src_ref=self.part(i, zz, 1 - self.c), dst_ref=self.sides[i].at[self.l, zz], send_sem=self.side_s.at[self.l, i, zz],
            recv_sem=self.side_r.at[self.l, i, zz], device_id=self.dev(self.z, 1 - self.c), device_id_type=MESH)

    def start(self):
        for k in range(self.chips):
            away = 0 if k == self.chips - 1 else -1 - k // 2 if k % 2 == 0 else 1 + k // 2
            for i, zz in ((0, self.chunk(0, k)), (1, self.chunk(1, k)), (2, (self.z + self.chips + away) % self.chips)):
                self.side(i, zz).start()
                self.local(i, zz).start()

    def ready(self, i, zz):
        self.local(i, zz).wait()
        self.side(i, zz).wait()

    def ring(self, way, j, k):
        ref = self.slots[way * 2 + j]
        to = (self.z + (1 if way == 0 else self.chips - 1)) % self.chips
        return pltpu.make_async_remote_copy(
            src_ref=ref.at[self.l, k], dst_ref=ref.at[self.l, k + 1], send_sem=self.ring_s.at[self.l, way * 2 + j, k],
            recv_sem=self.ring_r.at[self.l, way * 2 + j, k], device_id=self.dev(to, self.c), device_id_type=MESH)

    def step(self, k):
        for way in (0, 1):
            zz = self.chunk(way, k)
            for j in (0, 1):
                i = way if j == 0 else 2
                ref = self.slots[way * 2 + j]
                if j == 0:
                    self.ready(i, zz)
                    terms = self.own[i][self.l, zz].astype(F32) + self.sides[i][self.l, zz].astype(F32)
                else:
                    if 2 * k < self.chips - 1 if way == 0 else 2 * k < self.chips - 2:
                        self.ready(i, zz)
                    elif way == 0 and k == self.chips - 1:
                        self.ready(i, zz)
                    half = self.own[i].shape[-2] // 2
                    rows = pl.ds(way * half, half)
                    terms = self.own[i][self.l, zz, rows].astype(F32) + self.sides[i][self.l, zz, rows].astype(F32)
                if k > 0:
                    self.ring(way, j, k - 1).wait_recv()
                    terms = terms + ref[self.l, k].astype(F32)
                ref[self.l, k] = terms.astype(BF)
                if k < self.chips - 1:
                    self.ring(way, j, k).start()

    def finish(self):
        for way in (0, 1):
            for j in (0, 1):
                for k in range(self.chips - 1):
                    self.ring(way, j, k).wait_send()


def scatter_kernel(chips, layers, *refs):
    n = 3 * layers
    grads, outs, total = refs[:n], refs[n : n + 3], refs[n + 3]
    own, side, slots, mine, sems = refs[n + 4 : n + 7], refs[n + 7 : n + 10], refs[n + 10 : n + 14], refs[n + 14], refs[n + 15 : n + 20]
    sq_s, sq_r, pair, pair_sem = refs[n + 20 : n + 24]
    z, c, dev = place()
    others = [(z + k) % chips for k in range(1, chips)]
    greet([dev(o, c) for o in others] + [dev(z, 1 - c)])
    all_of = [Scatter(chips, l, grads[3 * l : 3 * l + 3], own, side, slots, sems) for l in reversed(range(layers))]
    for one in all_of:
        one.start()
    for k in range(chips):
        for one in all_of:
            one.step(k)
    squares = jnp.zeros((), F32)
    for l in range(layers):
        half = outs[2].shape[1] // 2
        for ref, out in ((slots[0], outs[0].at[l]), (slots[2], outs[1].at[l]), (slots[1], outs[2].at[l, :half]), (slots[3], outs[2].at[l, half:])):
            g = ref[l, chips - 1].astype(F32)
            out[...] = g
            squares = squares + jnp.sum(g * g)
    mine[0] = jnp.full(mine.shape[1:], squares, F32)
    copies = [
        pltpu.make_async_remote_copy(src_ref=mine.at[0], dst_ref=mine.at[k], send_sem=sq_s.at[k], recv_sem=sq_r.at[k], device_id=dev(o, c), device_id_type=MESH)
        for k, o in enumerate(others, 1)
    ]
    for copy in copies:
        copy.start()
    for copy in copies:
        copy.wait()
    pair[0] = jnp.sum(mine[...], 0)
    copy = pltpu.make_async_remote_copy(src_ref=pair.at[0], dst_ref=pair.at[1], send_sem=pair_sem.at[0], recv_sem=pair_sem.at[1], device_id=dev(z, 1 - c), device_id_type=MESH)
    copy.start()
    copy.wait()
    total[...] = pair[0] + pair[1]
    for one in all_of:
        one.finish()


def scatter_all(grads, n):
    layers, chips = len(grads) // 3, n // 2
    shapes = [(g.shape[0] // n, g.shape[1]) for g in grads[:3]]
    half = (shapes[2][0] // 2, shapes[2][1])
    sem = pltpu.SemaphoreType.DMA
    scratch = [pltpu.VMEM((layers, chips, *s), BF) for s in shapes] * 2
    scratch += [pltpu.VMEM((layers, chips, *s), BF) for s in (shapes[0], half, shapes[1], half)]
    scratch += [pltpu.VMEM((chips, 8, 128), F32)]
    scratch += [sem((layers, 3, chips))] * 3 + [sem((layers, 4, chips - 1))] * 2
    scratch += [sem((chips,))] * 2 + [pltpu.VMEM((2, 8, 128), F32), sem((2,))]
    return pl.pallas_call(
        functools.partial(scatter_kernel, chips, layers),
        out_shape=[jax.ShapeDtypeStruct((layers, *s), F32) for s in shapes] + [jax.ShapeDtypeStruct((8, 128), F32)],
        in_specs=[ANY] * (3 * layers),
        out_specs=[VM] * 4,
        scratch_shapes=scratch,
        compiler_params=pltpu.CompilerParams(collective_id=1, has_side_effects=True, vmem_limit_bytes=LIMIT),
        name="scatter",
    )(*grads)


def blocks(width):
    return [slice(i, i + COLS) for i in range(0, width, COLS)]


def forward_kernel(x_ref, wg, wu, wd, gate_ref, up_ref, h_ref):
    x = x_ref[0]
    _, _, a = norm_of(x)
    down = jnp.zeros(x.shape, F32)
    for cols in blocks(wg.shape[1]):
        gate, up = dot(a, wg[:, cols]), dot(a, wu[:, cols])
        gate_ref[:, cols], up_ref[:, cols] = gate, up
        act = (gate * jax.nn.sigmoid(gate) * up).astype(BF)
        down += dot(act, wd[cols, :])
    h_ref[0] = (x.astype(F32) + rounded(down)).astype(BF)


def add_to(acc, cols, value):
    @pl.when(pl.program_id(0) == 0)
    def _():
        acc[:, cols] = value

    @pl.when(pl.program_id(0) > 0)
    def _():
        acc[:, cols] += value


def gates_back(gate, up, by_act):
    sig = jax.nn.sigmoid(gate)
    silu = gate * sig
    act = (silu * up).astype(BF)
    by_up = (by_act * silu).astype(BF)
    by_gate = (by_act * up * (sig * (1.0 + gate * (1.0 - sig)))).astype(BF)
    return act, by_gate, by_up


def write_out(accs, outs):
    @pl.when(pl.program_id(0) == pl.num_programs(0) - 1)
    def _():
        outs[0][...] = accs[0][...].astype(BF)
        outs[1][...] = accs[1][...].astype(BF)
        outs[2][...] = accs[2][...].T.astype(BF)


def zero(accs):
    @pl.when(pl.program_id(0) == 0)
    def _():
        for acc in accs:
            acc[...] = jnp.zeros_like(acc)


def top_kernel(h_ref, dy_ref, wg, wu, wd, by_h_ref, og, ou, od, ag, au, ad):
    zero((ag, au, ad))
    by_y = dy_ref[0]
    wide, scale, a = norm_of(h_ref[0])
    a_t, by_y_t = a.T, by_y.T
    by_a_g, by_a_u = jnp.zeros(a.shape, F32), jnp.zeros(a.shape, F32)
    for cols in blocks(wg.shape[1]):
        gate, up = dot(a, wg[:, cols]), dot(a, wu[:, cols])
        by_act = rounded(dot(by_y, wd[cols, :], 1, 1))
        act, by_gate, by_up = gates_back(gate, up, by_act)
        ag[:, cols] += dot(a_t, by_gate)
        au[:, cols] += dot(a_t, by_up)
        ad[:, cols] += dot(by_y_t, act)
        by_a_g += dot(by_gate, wg[:, cols], 1, 1)
        by_a_u += dot(by_up, wu[:, cols], 1, 1)
    by_a = rounded(rounded(by_a_g) + rounded(by_a_u))
    by_scale = jnp.sum(by_a * wide, -1, keepdims=True)
    by_h = by_a * scale - wide * (by_scale * scale * scale * scale / wide.shape[-1])
    by_h_ref[0] = (by_y.astype(F32) + rounded(by_h)).astype(BF)
    write_out((ag, au, ad), (og, ou, od))


def bottom_kernel(x_ref, by_y_ref, gate_ref, up_ref, wd, og, ou, od, ag, au, ad):
    zero((ag, au, ad))
    by_y = by_y_ref[0]
    _, _, a = norm_of(x_ref[0])
    a_t, by_y_t = a.T, by_y.T
    for cols in blocks(gate_ref.shape[1]):
        by_act = rounded(dot(by_y, wd[cols, :], 1, 1))
        act, by_gate, by_up = gates_back(gate_ref[:, cols], up_ref[:, cols], by_act)
        ag[:, cols] += dot(a_t, by_gate)
        au[:, cols] += dot(a_t, by_up)
        ad[:, cols] += dot(by_y_t, act)
    write_out((ag, au, ad), (og, ou, od))


def tiles(width):
    return pl.BlockSpec((TILE, width), lambda t: (t, 0))


def states(width):
    return pl.BlockSpec((1, TILE, width), lambda t: (0, t, 0))


def whole(shape):
    return pl.BlockSpec(shape, lambda t: (0, 0), pipeline_mode=pl.Buffered(1))


def local_call(body, grid, in_specs, out_specs, out_shape, scratch, flops, name):
    return pl.pallas_call(
        body, grid=(grid,), in_specs=in_specs, out_specs=out_specs, out_shape=out_shape, scratch_shapes=scratch,
        cost_estimate=pl.CostEstimate(flops=flops, bytes_accessed=flops // 1000, transcendentals=0),
        compiler_params=pltpu.CompilerParams(dimension_semantics=("arbitrary",), vmem_limit_bytes=LIMIT), name=name)


def adamw(w, m, v, g):
    m = 0.9 * m + 0.1 * g
    v = 0.95 * v + 0.05 * g * g
    step = m * lax.rsqrt(v + 1e-8) + 0.1 * w
    return (w - 0.02 * step).astype(BF), m, v


def solution(mesh):
    n = mesh.shape["dp"]

    def step(x, dy, *arrays):
        weights, m, v = (arrays[i : i + 3] for i in (0, 3, 6))
        tokens, d = x.shape[1:]
        ff = weights[0].shape[2]
        grid = tokens // TILE
        flops = 2 * tokens * d * ff
        wg0, wu0, wd0, wg1, wu1, wd1 = gather_all(weights, n)
        state = jax.ShapeDtypeStruct(x.shape, BF)
        wide = jax.ShapeDtypeStruct((tokens, ff), F32)
        across, up_and_down = (d, ff), (ff, d)
        grads = [jax.ShapeDtypeStruct(s, BF) for s in (across, across, up_and_down)]
        accs = [pltpu.VMEM(across, F32)] * 3
        ws = [whole(across), whole(across), whole(up_and_down)]
        gate, up, h = local_call(
            forward_kernel, grid, [states(d)] + ws, [tiles(ff), tiles(ff), states(d)], [wide, wide, state], [], 3 * flops, "forward"
        )(x, wg0, wu0, wd0)
        by_h, *top = local_call(
            top_kernel, grid, [states(d), states(d)] + ws, [states(d)] + ws, [state] + grads, accs, 8 * flops, "top"
        )(h, dy, wg1, wu1, wd1)
        bottom = local_call(
            bottom_kernel, grid, [states(d), states(d), tiles(ff), tiles(ff), ws[2]], ws, grads, accs, 4 * flops, "bottom"
        )(x, by_h, gate, up, wd0)
        *mine, squares = scatter_all(list(bottom) + list(top), n)
        count = n * sum(g.size for g in mine)
        factor = jnp.minimum(1.0, 0.5 * lax.rsqrt(squares[0, 0] / count + 1e-30))
        new = [adamw(w.astype(F32), m, v, g * factor) for w, m, v, g in zip(weights, m, v, mine, strict=True)]
        return tuple(one[which] for which in range(3) for one in new)

    states_spec, cut = P(("rep", "dp"), None, None), P(None, "dp", None)
    return jax.shard_map(
        step,
        mesh=mesh,
        in_specs=(states_spec, states_spec) + (cut,) * 9,
        out_specs=(P("rep", "dp", None),) * 9,
        check_vma=False,
    )
```

profile of v0, /device:TPU:21, one launch (start us, length us, event | category | flops | bytes accessed | tf_op | source)
XLA Modules:
  0.0 333.1 jit_solution(17557254028939800207)
XLA Ops:
  0.6 69.7 %gather.1 = (bf16[640,1536]{1,0:T(8,128)(2,1)}, bf16[640,1536]{1,0:T(8,128)(2,1)}, bf16[1536,640]{1,0:T(8,128)(2,1)}, bf16[640,1536]{1,0:T(8,128)(2,1)}, bf16[64...) custom-call(bf16[2,40,1536]{2,1,0:T(8,128)(2,1)} %refs_0_.1, bf16[2,40,1536]{2,1,0:T(8,128)(2,1)} %refs_1_.1, ...), custom_call_target="tpu_custom_call" | custom-call | tf_op jit(solution)/shard_map/gather/pallas_call | solution.py:129
  70.3 37.9 %forward.1 = (f32[4096,1536]{1,0:T(8,128)}, f32[4096,1536]{1,0:T(8,128)}, bf16[1,4096,640]{2,1,0:T(8,128)(2,1)}) custom-call(bf16[1,4096,640]{2,1,0:T(8,128)(2,1)} %x_ref.3, bf16[640,1536]{1,0:T(8,128)(2,1)} %get-tuple-element.29.wg, bf16[640,1536]{1,0:T(8,128)(2,1)} %get-tuple-element.30.wu, bf16[1536,640]{1,0:T(8,128)(2,1)} %get-tuple-element.31.wd), custom_call_target="tpu_custom_call" | custom-call | flops 24159191040 | bytes 24159192 | tf_op jit(solution)/shard_map/forward/pallas_call | solution.py:399
  108.2 92.8 %top.1 = (bf16[1,4096,640]{2,1,0:T(8,128)(2,1)}, bf16[640,1536]{1,0:T(8,128)(2,1)}, bf16[640,1536]{1,0:T(8,128)(2,1)}, bf16[1536,640]{1,0:T(8,128)(2,1)}) custom-call(bf16[1,4096,640]{2,1,0:T(8,128)(2,1)} %get-tuple-element.32.h_ref, bf16[1,4096,640]{2,1,0:T(8,128)(2,1)} %dy_ref.1, bf16[640,1536]{1,0:T(8,128)(2,1)} %get-tuple-element.33.wg, ...), custom_call_target="tpu_custom_call" | custom-call | flops 64424509440 | bytes 64424508 | tf_op jit(solution)/shard_map/top/pallas_call | solution.py:402
  201.0 52.1 %bottom.1 = (bf16[640,1536]{1,0:T(8,128)(2,1)}, bf16[640,1536]{1,0:T(8,128)(2,1)}, bf16[1536,640]{1,0:T(8,128)(2,1)}) custom-call(bf16[1,4096,640]{2,1,0:T(8,128)(2,1)} %x_ref.3, bf16[1,4096,640]{2,1,0:T(8,128)(2,1)} %get-tuple-element.36.by_y_ref, f32[4096,1536]{1,0:T(8,128)} %get-tuple-element.37.gate_ref, f32[4096,1536]{1,0:T(8,128)} %get-tuple-element.38.up_ref, ...), custom_call_target="tpu_custom_call" | custom-call | flops 32212254720 | bytes 32212254 | tf_op jit(solution)/shard_map/bottom/pallas_call | solution.py:405
  253.1 0.0 copy-start.4
  253.1 72.9 %scatter.1 = (f32[2,40,1536]{2,1,0:T(8,128)}, f32[2,40,1536]{2,1,0:T(8,128)}, f32[2,96,640]{2,1,0:T(8,128)}, f32[8,128]{1,0:T(8,128)}) custom-call(bf16[640,1536]{1,0:T(8,128)(2,1)} %get-tuple-element.39.refs_0_, bf16[640,1536]{1,0:T(8,128)(2,1)} %get-tuple-element.40.refs_1_, bf16[1536,640]{1,0:T(8,128)(2,1)} %get-tuple-element.41.refs_2_, ...), custom_call_target="tpu_custom_call" | custom-call | tf_op jit(solution)/shard_map/scatter/pallas_call | solution.py:260
  326.0 0.0 copy-start.1
  326.0 0.0 copy-start.2
  326.0 0.0 copy-start.5
  326.1 0.0 copy-start.6
  326.1 0.0 copy-start.7
  326.1 0.0 copy-start.8
  326.1 0.0 copy-start.9
  326.1 1.3 slice.3
  328.1 0.0 copy-done
  328.2 0.0 copy-done.3
  328.2 0.0 copy-done.4
  328.2 2.2 fusion.8
  330.3 0.0 copy-done.1
  330.3 0.0 copy-done.2
  330.3 0.0 copy-done.5
  330.4 0.0 copy-done.6
  330.4 0.0 copy-done.7
  330.4 2.8 fusion.2
  (4 shorter events, 0.0 us)
Async XLA Ops:
  253.0 75.1 %copy-start = (bf16[2,96,640]{2,1,0:T(8,128)(2,1)S(1)}, bf16[2,96,640]{2,1,0:T(8,128)(2,1)}, u32[]{:S(2)}) copy-start(bf16[2,96,640]{2,1,0:T(8,128)(2,1)} %refs_2_.1) | copy-start | bytes 737284
  253.1 75.1 %copy-start.3 = (f32[2,96,640]{2,1,0:T(8,128)S(1)}, f32[2,96,640]{2,1,0:T(8,128)}, u32[]{:S(2)}) copy-start(f32[2,96,640]{2,1,0:T(8,128)} %param.21) | copy-start | bytes 1474564
  253.1 75.1 %copy-start.4 = (f32[2,96,640]{2,1,0:T(8,128)S(1)}, f32[2,96,640]{2,1,0:T(8,128)}, u32[]{:S(2)}) copy-start(f32[2,96,640]{2,1,0:T(8,128)} %param.18) | copy-start | bytes 1474564
  326.0 4.3 %copy-start.1 = (bf16[2,40,1536]{2,1,0:T(8,128)(2,1)S(1)}, bf16[2,40,1536]{2,1,0:T(8,128)(2,1)}, u32[]{:S(2)}) copy-start(bf16[2,40,1536]{2,1,0:T(8,128)(2,1)} %refs_0_.1) | copy-start | bytes 737284
  326.0 4.3 %copy-start.2 = (bf16[2,40,1536]{2,1,0:T(8,128)(2,1)S(1)}, bf16[2,40,1536]{2,1,0:T(8,128)(2,1)}, u32[]{:S(2)}) copy-start(bf16[2,40,1536]{2,1,0:T(8,128)(2,1)} %refs_1_.1) | copy-start | bytes 737284
  326.0 4.3 %copy-start.5 = (f32[2,40,1536]{2,1,0:T(8,128)S(1)}, f32[2,40,1536]{2,1,0:T(8,128)}, u32[]{:S(2)}) copy-start(f32[2,40,1536]{2,1,0:T(8,128)} %param.19) | copy-start | bytes 1474564
  326.1 4.3 %copy-start.6 = (f32[2,40,1536]{2,1,0:T(8,128)S(1)}, f32[2,40,1536]{2,1,0:T(8,128)}, u32[]{:S(2)}) copy-start(f32[2,40,1536]{2,1,0:T(8,128)} %param.16) | copy-start | bytes 1474564
  326.1 4.3 %copy-start.7 = (f32[2,40,1536]{2,1,0:T(8,128)S(1)}, f32[2,40,1536]{2,1,0:T(8,128)}, u32[]{:S(2)}) copy-start(f32[2,40,1536]{2,1,0:T(8,128)} %param.20) | copy-start | bytes 1474564
  326.1 4.3 %copy-start.8 = (f32[2,40,1536]{2,1,0:T(8,128)S(1)}, f32[2,40,1536]{2,1,0:T(8,128)}, u32[]{:S(2)}) copy-start(f32[2,40,1536]{2,1,0:T(8,128)} %param.17) | copy-start | bytes 1474564
  326.1 4.3 %copy-start.9 = (f32[2,40,1536]{2,1,0:T(8,128)S(1)}, f32[2,40,1536]{2,1,0:T(8,128)}, u32[]{:S(2)}) copy-start(f32[2,40,1536]{2,1,0:T(8,128)} %get-tuple-element.45) | copy-start | bytes 1474564
where the time goes:
time: 333 us
  Pallas kernels  325 us (98%)
  other arithmetic  4.92 us (1%)
    pallas_call x1, Pallas kernels, step(): local_call(top_kernel, grid, [states(d), states(d)] + ws, [states(d)] + w...  92.8 us
    pallas_call x1, Pallas kernels, scatter_all(): pl.pallas_call(functools.partial(scatter_kernel, chips, layers), out_shap...  72.9 us
    pallas_call x1, Pallas kernels, gather_all(): pl.pallas_call(functools.partial(gather_kernel, chips, layers), out_shape...  69.7 us
    pallas_call x1, Pallas kernels, step(): local_call(bottom_kernel, grid, [states(d), states(d), tiles(ff), tiles(f...  52.1 us
    pallas_call x1, Pallas kernels, step(): local_call(forward_kernel, grid, [states(d)] + ws, [tiles(ff), tiles(ff),...  37.9 us

commit v1 on v0

v1 whole, which is shorter than its diff:
```python
import functools

import jax
import jax.numpy as jnp
from jax import lax
from jax.experimental import pallas as pl
from jax.experimental.pallas import tpu as pltpu
from jax.sharding import PartitionSpec as P

MESH = pl.DeviceIdType.MESH
BF, F32 = jnp.bfloat16, jnp.float32
ANY = pl.BlockSpec(memory_space=pl.ANY)
VM = pl.BlockSpec(memory_space=pltpu.VMEM)
TILE = 512
COLS = 512
LIMIT = 60 * 1024 * 1024
MOVES = (0, 1, 2, 4, 6, 8, 9, 11)


def dot(a, b, ca=1, cb=0):
    return lax.dot_general(a, b, (((ca,), (cb,)), ((), ())), preferred_element_type=F32)


def rounded(a):
    return a.astype(BF).astype(F32)


def norm_of(h):
    wide = h.astype(F32)
    scale = lax.rsqrt(jnp.mean(wide * wide, -1, keepdims=True) + 1e-6)
    return wide, scale, (wide * scale).astype(BF)


def place():
    me = lax.axis_index("dp")
    z, c = me // 2, me % 2
    return z, c, lambda zz, cc: {"dp": zz * 2 + cc}


def greet(peers):
    barrier = pltpu.get_barrier_semaphore()
    for p in peers:
        pl.semaphore_signal(barrier, inc=1, device_id=p, device_id_type=MESH)
    pl.semaphore_wait(barrier, len(peers))


def reach(m, chips):
    far, near = chips // 2, chips - 1 - chips // 2
    return (far, near) if m % 2 == 0 else (near, far)


class Gather:
    def __init__(self, chips, m, hops, src, out, sems):
        self.chips, self.m, self.hops, self.src, self.out = chips, m, hops, src, out
        self.ring_s, self.ring_r, self.side_s, self.side_r, self.own = sems
        self.rows = src.shape[0]
        self.z, self.c, self.dev = place()

    def at(self, zz, cc):
        return self.out.at[pl.ds(pl.multiple_of((zz * 2 + cc) * self.rows, 8), self.rows)]

    def ring(self, way, k, src=None):
        step = 1 if way == 0 else -1
        origin = (self.z - step * k + self.chips) % self.chips
        to = (self.z + step + self.chips) % self.chips
        block = self.at(origin, self.c)
        i = (0 if way == 0 else self.hops[0]) + k
        return pltpu.make_async_remote_copy(
            src_ref=block if src is None else src, dst_ref=block, send_sem=self.ring_s.at[self.m, i], recv_sem=self.ring_r.at[self.m, i],
            device_id=self.dev(to, self.c), device_id_type=MESH)

    def side(self, origin, i, src=None):
        block = self.at(origin, self.c)
        return pltpu.make_async_remote_copy(
            src_ref=block if src is None else src, dst_ref=block, send_sem=self.side_s.at[self.m, i], recv_sem=self.side_r.at[self.m, i],
            device_id=self.dev(self.z, 1 - self.c), device_id_type=MESH)

    def keep(self):
        return pltpu.make_async_copy(self.src, self.at(self.z, self.c), self.own.at[self.m])

    def start(self):
        for way in (0, 1):
            self.ring(way, 0, self.src).start()
        self.side(self.z, 0, self.src).start()
        self.keep().start()

    def step(self, k):
        for way in (0, 1):
            if k > self.hops[way]:
                continue
            self.ring(way, k - 1).wait_recv()
            if k < self.hops[way]:
                self.ring(way, k).start()
            origin = (self.z - (1 if way == 0 else -1) * k + self.chips) % self.chips
            self.side(origin, k + (0 if way == 0 else self.hops[0])).start()

    def finish(self):
        for way in (0, 1):
            for k in range(self.hops[way]):
                self.ring(way, k).wait_send()
        for i in range(self.chips):
            self.side(self.z, i).wait()
        self.keep().wait()


def gather_sems(n, chips):
    return [pltpu.SemaphoreType.DMA((n, chips - 1))] * 2 + [pltpu.SemaphoreType.DMA((n, chips))] * 2 + [pltpu.SemaphoreType.DMA((n,))]


def gathers(chips, layer, shards, outs, sems):
    z, c, dev = place()
    peers = [dev((z + 1) % chips, c), dev((z + chips - 1) % chips, c), dev(z, 1 - c)]
    return peers, [Gather(chips, i, reach(i + layer, chips), shards[i].at[layer], outs[i], sems) for i in range(3)]


def gather_kernel(chips, *refs):
    peers, all_of = gathers(chips, 0, refs[:3], refs[3:6], refs[6:])
    greet(peers)
    for one in all_of:
        one.start()
    for k in range(1, chips // 2 + 1):
        for one in all_of:
            one.step(k)
    for one in all_of:
        one.finish()


def gathered(weights, n):
    return [jax.ShapeDtypeStruct((w.shape[1] * n, w.shape[2]), w.dtype) for w in weights]


def gather_first(weights, n):
    chips = n // 2
    return pl.pallas_call(
        functools.partial(gather_kernel, chips),
        out_shape=gathered(weights, n),
        in_specs=[VM] * 3,
        out_specs=[ANY] * 3,
        scratch_shapes=gather_sems(3, chips),
        compiler_params=pltpu.CompilerParams(collective_id=0, has_side_effects=True),
        name="gather",
    )(*weights)


class Scatter:
    def __init__(self, chips, grads, scratch):
        self.chips, self.grads = chips, grads
        self.own, self.sides, self.slots = scratch[:3], scratch[3:6], scratch[6:10]
        self.own_sem, self.side_s, self.side_r, self.ring_s, self.ring_r = scratch[10:15]
        self.z, self.c, self.dev = place()
        self.peers = [self.dev((self.z + 1) % chips, self.c), self.dev((self.z + chips - 1) % chips, self.c), self.dev(self.z, 1 - self.c)]

    def part(self, i, zz, cc):
        rows = self.own[i].shape[-2]
        return self.grads[i].at[pl.ds(pl.multiple_of((zz * 2 + cc) * rows, 8), rows)]

    def chunk(self, way, k):
        return (self.z - 1 - k + 2 * self.chips) % self.chips if way == 0 else (self.z + 1 + k) % self.chips

    def local(self, i, zz):
        return pltpu.make_async_copy(self.part(i, zz, self.c), self.own[i].at[zz], self.own_sem.at[i, zz])

    def side(self, i, zz):
        return pltpu.make_async_remote_copy(
            src_ref=self.part(i, zz, 1 - self.c), dst_ref=self.sides[i].at[zz], send_sem=self.side_s.at[i, zz],
            recv_sem=self.side_r.at[i, zz], device_id=self.dev(self.z, 1 - self.c), device_id_type=MESH)

    def start(self):
        for k in range(self.chips):
            away = 0 if k == self.chips - 1 else -1 - k // 2 if k % 2 == 0 else 1 + k // 2
            for i, zz in ((0, self.chunk(0, k)), (1, self.chunk(1, k)), (2, (self.z + self.chips + away) % self.chips)):
                self.side(i, zz).start()
                self.local(i, zz).start()

    def ready(self, i, zz):
        self.local(i, zz).wait()
        self.side(i, zz).wait()

    def ring(self, way, j, k):
        ref = self.slots[way * 2 + j]
        to = (self.z + (1 if way == 0 else self.chips - 1)) % self.chips
        return pltpu.make_async_remote_copy(
            src_ref=ref.at[k], dst_ref=ref.at[k + 1], send_sem=self.ring_s.at[way * 2 + j, k],
            recv_sem=self.ring_r.at[way * 2 + j, k], device_id=self.dev(to, self.c), device_id_type=MESH)

    def step(self, k):
        for way in (0, 1):
            zz = self.chunk(way, k)
            for j in (0, 1):
                i = way if j == 0 else 2
                ref = self.slots[way * 2 + j]
                if j == 0:
                    self.ready(i, zz)
                    terms = self.own[i][zz].astype(F32) + self.sides[i][zz].astype(F32)
                else:
                    if 2 * k < self.chips - 1 if way == 0 else 2 * k < self.chips - 2:
                        self.ready(i, zz)
                    elif way == 0 and k == self.chips - 1:
                        self.ready(i, zz)
                    half = self.own[i].shape[-2] // 2
                    rows = pl.ds(way * half, half)
                    terms = self.own[i][zz, rows].astype(F32) + self.sides[i][zz, rows].astype(F32)
                if k > 0:
                    self.ring(way, j, k - 1).wait_recv()
                    terms = terms + ref[k].astype(F32)
                ref[k] = terms.astype(BF)
                if k < self.chips - 1:
                    self.ring(way, j, k).start()

    def finish(self):
        for way in (0, 1):
            for j in (0, 1):
                for k in range(self.chips - 1):
                    self.ring(way, j, k).wait_send()


    def blocks(self):
        last, half = self.chips - 1, self.own[2].shape[-2] // 2
        return (0, slice(None), self.slots[0][last]), (1, slice(None), self.slots[2][last]), (2, slice(0, half), self.slots[1][last]), (2, slice(half, None), self.slots[3][last])


def block_shapes(grads, n):
    return [(g.shape[0] // n, g.shape[1]) for g in grads]


def scatter_scratch(shapes, chips):
    half = (shapes[2][0] // 2, shapes[2][1])
    sem = pltpu.SemaphoreType.DMA
    scratch = [pltpu.VMEM((chips, *s), BF) for s in shapes] * 2
    scratch += [pltpu.VMEM((chips, *s), BF) for s in (shapes[0], half, shapes[1], half)]
    return scratch + [sem((3, chips))] * 3 + [sem((4, chips - 1))] * 2


def scatter_kernel(chips, *refs):
    grads, done, outs, total = refs[:3], refs[3:6], refs[6:9], refs[9]
    mine, sq_s, sq_r, pair, pair_sem = refs[25:]
    z, c, dev = place()
    others = [(z + k) % chips for k in range(1, chips)]
    greet([dev(o, c) for o in others] + [dev(z, 1 - c)])
    one = Scatter(chips, grads, refs[10:25])
    one.start()
    squares = jnp.zeros((), F32)
    for k in range(chips):
        one.step(k)
        if k < 3:
            g = done[k][...].astype(F32)
            outs[k][1] = g
            squares += jnp.sum(g * g)
    for i, rows, g in one.blocks():
        g = g.astype(F32)
        outs[i][0, rows] = g
        squares += jnp.sum(g * g)
    mine[0] = jnp.full(mine.shape[1:], squares, F32)
    copies = [
        pltpu.make_async_remote_copy(src_ref=mine.at[0], dst_ref=mine.at[k], send_sem=sq_s.at[k], recv_sem=sq_r.at[k], device_id=dev(o, c), device_id_type=MESH)
        for k, o in enumerate(others, 1)
    ]
    for copy in copies:
        copy.start()
    for copy in copies:
        copy.wait()
    pair[0] = jnp.sum(mine[...], 0)
    copy = pltpu.make_async_remote_copy(src_ref=pair.at[0], dst_ref=pair.at[1], send_sem=pair_sem.at[0], recv_sem=pair_sem.at[1], device_id=dev(z, 1 - c), device_id_type=MESH)
    copy.start()
    copy.wait()
    total[...] = pair[0] + pair[1]
    one.finish()


def scatter_last(grads, done, n):
    chips = n // 2
    shapes = block_shapes(grads, n)
    sem = pltpu.SemaphoreType.DMA
    return pl.pallas_call(
        functools.partial(scatter_kernel, chips),
        out_shape=[jax.ShapeDtypeStruct((2, *s), F32) for s in shapes] + [jax.ShapeDtypeStruct((8, 128), F32)],
        in_specs=[ANY] * 3 + [VM] * 3,
        out_specs=[VM] * 4,
        scratch_shapes=scatter_scratch(shapes, chips) + [pltpu.VMEM((chips, 8, 128), F32), sem((chips,)), sem((chips,)), pltpu.VMEM((2, 8, 128), F32), sem((2,))],
        compiler_params=pltpu.CompilerParams(collective_id=1, has_side_effects=True, vmem_limit_bytes=LIMIT),
        name="scatter",
    )(*grads, *done)


def blocks(width):
    return [slice(i, i + COLS) for i in range(0, width, COLS)]


def forward_kernel(chips, x_ref, wg, wu, wd, *refs):
    shards, (gate_ref, up_ref, h_ref), outs, sems = refs[:3], refs[3:6], refs[6:9], refs[9:]
    t, last = pl.program_id(0), pl.num_programs(0) - 1
    peers, all_of = gathers(chips, 1, shards, outs, sems)
    moves = [(one, k) for k in range(1, chips // 2 + 1) for one in all_of]

    @pl.when(t == 0)
    def _():
        greet(peers)
        for one in all_of:
            one.start()

    for at, (begin, end) in enumerate(zip(MOVES, MOVES[1:]), 1):
        @pl.when(t == at)
        def _():
            for one, k in moves[begin:end]:
                one.step(k)

    x = x_ref[0]
    _, _, a = norm_of(x)
    down = jnp.zeros(x.shape, F32)
    for cols in blocks(wg.shape[1]):
        gate, up = dot(a, wg[:, cols]), dot(a, wu[:, cols])
        gate_ref[:, cols], up_ref[:, cols] = gate, up
        act = (gate * jax.nn.sigmoid(gate) * up).astype(BF)
        down += dot(act, wd[cols, :])
    h_ref[0] = (x.astype(F32) + rounded(down)).astype(BF)

    @pl.when(t == last)
    def _():
        for one, k in moves[MOVES[-1]:]:
            one.step(k)
        for one in all_of:
            one.finish()


def gates_back(gate, up, by_act):
    sig = jax.nn.sigmoid(gate)
    silu = gate * sig
    act = (silu * up).astype(BF)
    by_up = (by_act * silu).astype(BF)
    by_gate = (by_act * up * (sig * (1.0 + gate * (1.0 - sig)))).astype(BF)
    return act, by_gate, by_up


def write_out(accs, outs):
    @pl.when(pl.program_id(0) == pl.num_programs(0) - 1)
    def _():
        outs[0][...] = accs[0][...].astype(BF)
        outs[1][...] = accs[1][...].astype(BF)
        outs[2][...] = accs[2][...].T.astype(BF)


def zero(accs):
    @pl.when(pl.program_id(0) == 0)
    def _():
        for acc in accs:
            acc[...] = jnp.zeros_like(acc)


def top_kernel(h_ref, dy_ref, wg, wu, wd, by_h_ref, og, ou, od, ag, au, ad):
    zero((ag, au, ad))
    by_y = dy_ref[0]
    wide, scale, a = norm_of(h_ref[0])
    a_t, by_y_t = a.T, by_y.T
    by_a_g, by_a_u = jnp.zeros(a.shape, F32), jnp.zeros(a.shape, F32)
    for cols in blocks(wg.shape[1]):
        gate, up = dot(a, wg[:, cols]), dot(a, wu[:, cols])
        by_act = rounded(dot(by_y, wd[cols, :], 1, 1))
        act, by_gate, by_up = gates_back(gate, up, by_act)
        ag[:, cols] += dot(a_t, by_gate)
        au[:, cols] += dot(a_t, by_up)
        ad[:, cols] += dot(by_y_t, act)
        by_a_g += dot(by_gate, wg[:, cols], 1, 1)
        by_a_u += dot(by_up, wu[:, cols], 1, 1)
    by_a = rounded(rounded(by_a_g) + rounded(by_a_u))
    by_scale = jnp.sum(by_a * wide, -1, keepdims=True)
    by_h = by_a * scale - wide * (by_scale * scale * scale * scale / wide.shape[-1])
    by_h_ref[0] = (by_y.astype(F32) + rounded(by_h)).astype(BF)
    write_out((ag, au, ad), (og, ou, od))


def bottom_kernel(chips, x_ref, by_y_ref, gate_ref, up_ref, wd, *refs):
    top, (og, ou, od), done, (ag, au, ad) = refs[:3], refs[3:6], refs[6:9], refs[9:12]
    t, last = pl.program_id(0), pl.num_programs(0) - 1
    one = Scatter(chips, top, refs[12:])

    @pl.when(t == 0)
    def _():
        greet(one.peers)
        one.start()

    for k in range(chips - 1):
        @pl.when(t == k + 1)
        def _():
            one.step(k)

    zero((ag, au, ad))
    by_y = by_y_ref[0]
    _, _, a = norm_of(x_ref[0])
    a_t, by_y_t = a.T, by_y.T
    for cols in blocks(gate_ref.shape[1]):
        by_act = rounded(dot(by_y, wd[cols, :], 1, 1))
        act, by_gate, by_up = gates_back(gate_ref[:, cols], up_ref[:, cols], by_act)
        ag[:, cols] += dot(a_t, by_gate)
        au[:, cols] += dot(a_t, by_up)
        ad[:, cols] += dot(by_y_t, act)
    write_out((ag, au, ad), (og, ou, od))

    @pl.when(t == last)
    def _():
        one.step(chips - 1)
        for i, rows, g in one.blocks():
            done[i][rows] = g
        one.finish()


def tiles(width):
    return pl.BlockSpec((TILE, width), lambda t: (t, 0))


def states(width):
    return pl.BlockSpec((1, TILE, width), lambda t: (0, t, 0))


def whole(shape):
    return pl.BlockSpec(shape, lambda t: (0,) * len(shape), pipeline_mode=pl.Buffered(1))


def tiled_call(body, grid, in_specs, out_specs, out_shape, scratch, flops, name, **more):
    return pl.pallas_call(
        body, grid=(grid,), in_specs=in_specs, out_specs=out_specs, out_shape=out_shape, scratch_shapes=scratch,
        cost_estimate=pl.CostEstimate(flops=flops, bytes_accessed=flops // 1000, transcendentals=0),
        compiler_params=pltpu.CompilerParams(dimension_semantics=("arbitrary",), vmem_limit_bytes=LIMIT, **more), name=name)


def adamw(w, m, v, g):
    m = 0.9 * m + 0.1 * g
    v = 0.95 * v + 0.05 * g * g
    step = m * lax.rsqrt(v + 1e-8) + 0.1 * w
    return (w - 0.02 * step).astype(BF), m, v


def solution(mesh):
    n = mesh.shape["dp"]

    def step(x, dy, *arrays):
        weights, m, v = (arrays[i : i + 3] for i in (0, 3, 6))
        tokens, d = x.shape[1:]
        ff = weights[0].shape[2]
        grid = tokens // TILE
        flops = 2 * tokens * d * ff
        chips = n // 2
        assert grid == chips
        wg0, wu0, wd0 = gather_first(weights, n)
        state = jax.ShapeDtypeStruct(x.shape, BF)
        wide = jax.ShapeDtypeStruct((tokens, ff), F32)
        across, up_and_down = (d, ff), (ff, d)
        grads = [jax.ShapeDtypeStruct(s, BF) for s in (across, across, up_and_down)]
        accs = [pltpu.VMEM(across, F32)] * 3
        ws = [whole(across), whole(across), whole(up_and_down)]
        gate, up, h, *next_w = tiled_call(
            functools.partial(forward_kernel, chips), grid, [states(d)] + ws + [whole(w.shape) for w in weights],
            [tiles(ff), tiles(ff), states(d)] + [ANY] * 3, [wide, wide, state] + gathered(weights, n), gather_sems(3, chips), 3 * flops, "forward",
            collective_id=2, has_side_effects=True,
        )(x, wg0, wu0, wd0, *weights)
        by_h, *top = tiled_call(
            top_kernel, grid, [states(d), states(d)] + ws, [states(d)] + ws, [state] + grads, accs, 8 * flops, "top"
        )(h, dy, *next_w)
        shapes = block_shapes(grads, n)
        *bottom, b0, b1, b2 = tiled_call(
            functools.partial(bottom_kernel, chips), grid, [states(d), states(d), tiles(ff), tiles(ff), ws[2]] + [ANY] * 3,
            ws + [whole(b) for b in shapes], grads + [jax.ShapeDtypeStruct(b, BF) for b in shapes],
            accs + scatter_scratch(shapes, chips), 4 * flops, "bottom", collective_id=3, has_side_effects=True,
        )(x, by_h, gate, up, wd0, *top)
        *mine, squares = scatter_last(bottom, (b0, b1, b2), n)
        count = n * sum(g.size for g in mine)
        factor = jnp.minimum(1.0, 0.5 * lax.rsqrt(squares[0, 0] / count + 1e-30))
        new = [adamw(w.astype(F32), m, v, g * factor) for w, m, v, g in zip(weights, m, v, mine, strict=True)]
        return tuple(one[which] for which in range(3) for one in new)

    states_spec, cut = P(("rep", "dp"), None, None), P(None, "dp", None)
    return jax.shard_map(
        step,
        mesh=mesh,
        in_specs=(states_spec, states_spec) + (cut,) * 9,
        out_specs=(P("rep", "dp", None),) * 9,
        check_vma=False,
    )
```

time: 333 us -> 299 us (0.90)
  Pallas kernels: 325 us -> 291 us
    pallas_call x5, Pallas kernels: 325 us -> 291 us  [the longest x1 92.9 us: step(): tiled_call(top_kernel, grid, [states(d), states(d)] + ws, [states(d)] + w...]
where the time goes in v1:
time: 299 us; the launch traced here: 298 us
  Pallas kernels  291 us (97%)
  other arithmetic  4.92 us (2%)
    pallas_call x1, Pallas kernels, step(): tiled_call(top_kernel, grid, [states(d), states(d)] + ws, [states(d)] + w...  92.9 us
    pallas_call x1, Pallas kernels, step(): tiled_call(functools.partial(bottom_kernel, chips), grid, [states(d), sta...  58.2 us
    pallas_call x1, Pallas kernels, scatter_last(): pl.pallas_call(functools.partial(scatter_kernel, chips), out_shape=[jax.S...  50 us
    pallas_call x1, Pallas kernels, step(): tiled_call(functools.partial(forward_kernel, chips), grid, [states(d)] +...  47.1 us
    pallas_call x1, Pallas kernels, gather_first(): pl.pallas_call(functools.partial(gather_kernel, chips), out_shape=gathere...  42.5 us

profile of v1, /device:TPU:21, one launch (start us, length us, event | category | flops | bytes accessed | tf_op | source)
XLA Modules:
  0.0 298.4 jit_solution(2236032072497199653)
XLA Ops:
  0.6 42.5 %gather.1 = (bf16[640,1536]{1,0:T(8,128)(2,1)}, bf16[640,1536]{1,0:T(8,128)(2,1)}, bf16[1536,640]{1,0:T(8,128)(2,1)}) custom-call(bf16[2,40,1536]{2,1,0:T(8,128)(2,1)} %refs_0_.3, bf16[2,40,1536]{2,1,0:T(8,128)(2,1)} %refs_1_.3, bf16[2,96,640]{2,1,0:T(8,128)(2,1)} %refs_2_.3), custom_call_target="tpu_custom_call" | custom-call | tf_op jit(solution)/shard_map/gather/pallas_call | solution.py:134
  43.1 47.1 %forward.1 = (f32[4096,1536]{1,0:T(8,128)}, f32[4096,1536]{1,0:T(8,128)}, bf16[1,4096,640]{2,1,0:T(8,128)(2,1)}, bf16[640,1536]{1,0:T(8,128)(2,1)}, bf16[640,153...) custom-call(bf16[1,4096,640]{2,1,0:T(8,128)(2,1)} %x_ref.3, bf16[640,1536]{1,0:T(8,128)(2,1)} %get-tuple-element.32.wg, ...), custom_call_target="tpu_custom_call" | custom-call | flops 24159191040 | bytes 24159192 | tf_op jit(solution)/shard_map/forward/pallas_call | solution.py:450
  90.2 92.9 %top.1 = (bf16[1,4096,640]{2,1,0:T(8,128)(2,1)}, bf16[640,1536]{1,0:T(8,128)(2,1)}, bf16[640,1536]{1,0:T(8,128)(2,1)}, bf16[1536,640]{1,0:T(8,128)(2,1)}) custom-call(bf16[1,4096,640]{2,1,0:T(8,128)(2,1)} %get-tuple-element.35.h_ref, bf16[1,4096,640]{2,1,0:T(8,128)(2,1)} %dy_ref.1, bf16[640,1536]{1,0:T(8,128)(2,1)} %get-tuple-element.36.wg, ...), custom_call_target="tpu_custom_call" | custom-call | flops 64424509440 | bytes 64424508 | tf_op jit(solution)/shard_map/top/pallas_call | solution.py:455
  183.1 58.2 %bottom.1 = (bf16[640,1536]{1,0:T(8,128)(2,1)}, bf16[640,1536]{1,0:T(8,128)(2,1)}, bf16[1536,640]{1,0:T(8,128)(2,1)}, bf16[40,1536]{1,0:T(8,128)(2,1)}, bf16[40,...) custom-call(bf16[1,4096,640]{2,1,0:T(8,128)(2,1)} %x_ref.3, bf16[1,4096,640]{2,1,0:T(8,128)(2,1)} %get-tuple-element.39.by_y_ref, ...), custom_call_target="tpu_custom_call" | custom-call | flops 32212254720 | bytes 32212254 | tf_op jit(solution)/shard_map/bottom/pallas_call | solution.py:459
  241.3 0.0 copy-start
  241.3 0.0 copy-start.3
  241.3 0.0 copy-start.4
  241.3 50.0 %scatter.1 = (f32[2,40,1536]{2,1,0:T(8,128)}, f32[2,40,1536]{2,1,0:T(8,128)}, f32[2,96,640]{2,1,0:T(8,128)}, f32[8,128]{1,0:T(8,128)}) custom-call(bf16[640,1536]{1,0:T(8,128)(2,1)} %get-tuple-element.45.refs_0_, bf16[640,1536]{1,0:T(8,128)(2,1)} %get-tuple-element.46.refs_1_, bf16[1536,640]{1,0:T(8,128)(2,1)} %get-tuple-element.47.refs_2_, ...), custom_call_target="tpu_custom_call" | custom-call | tf_op jit(solution)/shard_map/scatter/pallas_call | solution.py:274
  291.3 0.0 copy-start.1
  291.3 0.0 copy-start.2
  291.3 0.0 copy-start.5
  291.3 0.0 copy-start.6
  291.4 0.0 copy-start.7
  291.4 0.0 copy-start.8
  291.4 0.0 copy-start.9
  291.4 1.3 slice.3
  293.4 0.0 copy-done
  293.4 0.0 copy-done.3
  293.5 2.2 fusion.8
  295.6 0.0 copy-done.6
  295.6 0.0 copy-done.7
  295.7 0.0 copy-done.8
  295.7 0.0 copy-done.9
  295.7 2.8 fusion.2
  (4 shorter events, 0.0 us)
Async XLA Ops:
  241.3 52.1 %copy-start = (bf16[2,96,640]{2,1,0:T(8,128)(2,1)S(1)}, bf16[2,96,640]{2,1,0:T(8,128)(2,1)}, u32[]{:S(2)}) copy-start(bf16[2,96,640]{2,1,0:T(8,128)(2,1)} %refs_2_.3) | copy-start | bytes 737284
  241.3 52.1 %copy-start.3 = (f32[2,96,640]{2,1,0:T(8,128)S(1)}, f32[2,96,640]{2,1,0:T(8,128)}, u32[]{:S(2)}) copy-start(f32[2,96,640]{2,1,0:T(8,128)} %param.21) | copy-start | bytes 1474564
  241.3 52.1 %copy-start.4 = (f32[2,96,640]{2,1,0:T(8,128)S(1)}, f32[2,96,640]{2,1,0:T(8,128)}, u32[]{:S(2)}) copy-start(f32[2,96,640]{2,1,0:T(8,128)} %param.18) | copy-start | bytes 1474564
  291.3 4.3 %copy-start.1 = (bf16[2,40,1536]{2,1,0:T(8,128)(2,1)S(1)}, bf16[2,40,1536]{2,1,0:T(8,128)(2,1)}, u32[]{:S(2)}) copy-start(bf16[2,40,1536]{2,1,0:T(8,128)(2,1)} %refs_0_.3) | copy-start | bytes 737284
  291.3 4.3 %copy-start.2 = (bf16[2,40,1536]{2,1,0:T(8,128)(2,1)S(1)}, bf16[2,40,1536]{2,1,0:T(8,128)(2,1)}, u32[]{:S(2)}) copy-start(bf16[2,40,1536]{2,1,0:T(8,128)(2,1)} %refs_1_.3) | copy-start | bytes 737284
  291.3 4.3 %copy-start.5 = (f32[2,40,1536]{2,1,0:T(8,128)S(1)}, f32[2,40,1536]{2,1,0:T(8,128)}, u32[]{:S(2)}) copy-start(f32[2,40,1536]{2,1,0:T(8,128)} %param.19) | copy-start | bytes 1474564
  291.3 4.3 %copy-start.6 = (f32[2,40,1536]{2,1,0:T(8,128)S(1)}, f32[2,40,1536]{2,1,0:T(8,128)}, u32[]{:S(2)}) copy-start(f32[2,40,1536]{2,1,0:T(8,128)} %param.16) | copy-start | bytes 1474564
  291.4 4.3 %copy-start.7 = (f32[2,40,1536]{2,1,0:T(8,128)S(1)}, f32[2,40,1536]{2,1,0:T(8,128)}, u32[]{:S(2)}) copy-start(f32[2,40,1536]{2,1,0:T(8,128)} %param.20) | copy-start | bytes 1474564
  291.4 4.3 %copy-start.8 = (f32[2,40,1536]{2,1,0:T(8,128)S(1)}, f32[2,40,1536]{2,1,0:T(8,128)}, u32[]{:S(2)}) copy-start(f32[2,40,1536]{2,1,0:T(8,128)} %param.17) | copy-start | bytes 1474564
  291.4 4.3 %copy-start.9 = (f32[2,40,1536]{2,1,0:T(8,128)S(1)}, f32[2,40,1536]{2,1,0:T(8,128)}, u32[]{:S(2)}) copy-start(f32[2,40,1536]{2,1,0:T(8,128)} %get-tuple-element.51) | copy-start | bytes 1474564

commit v2 on v1

--- a/solution.py
+++ b/solution.py
@@ -12,9 +12,10 @@
 ANY = pl.BlockSpec(memory_space=pl.ANY)
 VM = pl.BlockSpec(memory_space=pltpu.VMEM)
 TILE = 512
-COLS = 512
+TILE_FORWARD = 256
+COLS = 768
 LIMIT = 60 * 1024 * 1024
-MOVES = (0, 1, 2, 4, 6, 8, 9, 11)
+MOVES = (0, 0, 0, 1, 2, 3, 3, 4, 5, 6, 7, 7, 8, 9, 10, 11)
 
 
 def dot(a, b, ca=1, cb=0):
@@ -145,8 +146,8 @@
 class Scatter:
     def __init__(self, chips, grads, scratch):
         self.chips, self.grads = chips, grads
-        self.own, self.sides, self.slots = scratch[:3], scratch[3:6], scratch[6:10]
-        self.own_sem, self.side_s, self.side_r, self.ring_s, self.ring_r = scratch[10:15]
+        self.own, self.sides, self.slots = scratch[:3], scratch[3:6], scratch[6:12]
+        self.own_sem, self.side_s, self.side_r, self.ring_s, self.ring_r = scratch[12:17]
         self.z, self.c, self.dev = place()
         self.peers = [self.dev((self.z + 1) % chips, self.c), self.dev((self.z + chips - 1) % chips, self.c), self.dev(self.z, 1 - self.c)]
 
@@ -176,30 +177,28 @@
         self.local(i, zz).wait()
         self.side(i, zz).wait()
 
+    def pieces(self, way):
+        width, height = self.own[way].shape[-1] // 2, self.own[2].shape[-2] // 2
+        every = slice(None)
+        return (way, every, slice(0, width)), (way, every, slice(width, None)), (2, slice(way * height, way * height + height), every)
+
     def ring(self, way, j, k):
-        ref = self.slots[way * 2 + j]
+        ref = self.slots[way * 3 + j]
         to = (self.z + (1 if way == 0 else self.chips - 1)) % self.chips
         return pltpu.make_async_remote_copy(
-            src_ref=ref.at[k], dst_ref=ref.at[k + 1], send_sem=self.ring_s.at[way * 2 + j, k],
-            recv_sem=self.ring_r.at[way * 2 + j, k], device_id=self.dev(to, self.c), device_id_type=MESH)
+            src_ref=ref.at[k], dst_ref=ref.at[k + 1], send_sem=self.ring_s.at[way * 3 + j, k],
+            recv_sem=self.ring_r.at[way * 3 + j, k], device_id=self.dev(to, self.c), device_id_type=MESH)
 
     def step(self, k):
-        for way in (0, 1):
-            zz = self.chunk(way, k)
-            for j in (0, 1):
-                i = way if j == 0 else 2
-                ref = self.slots[way * 2 + j]
-                if j == 0:
+        for j in range(3):
+            for way in (0, 1):
+                zz = self.chunk(way, k)
+                i, rows, cols = self.pieces(way)[j]
+                first = 2 * k < self.chips - 1 or k == self.chips - 1 if way == 0 else 2 * k < self.chips - 2
+                if j == 0 or j == 2 and first:
                     self.ready(i, zz)
-                    terms = self.own[i][zz].astype(F32) + self.sides[i][zz].astype(F32)
-                else:
-                    if 2 * k < self.chips - 1 if way == 0 else 2 * k < self.chips - 2:
-                        self.ready(i, zz)
-                    elif way == 0 and k == self.chips - 1:
-                        self.ready(i, zz)
-                    half = self.own[i].shape[-2] // 2
-                    rows = pl.ds(way * half, half)
-                    terms = self.own[i][zz, rows].astype(F32) + self.sides[i][zz, rows].astype(F32)
+                ref = self.slots[way * 3 + j]
+                terms = self.own[i][zz, rows, cols].astype(F32) + self.sides[i][zz, rows, cols].astype(F32)
                 if k > 0:
                     self.ring(way, j, k - 1).wait_recv()
                     terms = terms + ref[k].astype(F32)
@@ -209,14 +208,12 @@
 
     def finish(self):
         for way in (0, 1):
-            for j in (0, 1):
+            for j in range(3):
                 for k in range(self.chips - 1):
                     self.ring(way, j, k).wait_send()
 
-
     def blocks(self):
-        last, half = self.chips - 1, self.own[2].shape[-2] // 2
-        return (0, slice(None), self.slots[0][last]), (1, slice(None), self.slots[2][last]), (2, slice(0, half), self.slots[1][last]), (2, slice(half, None), self.slots[3][last])
+        return [(*piece, self.slots[way * 3 + j][self.chips - 1]) for way in (0, 1) for j, piece in enumerate(self.pieces(way))]
 
 
 def block_shapes(grads, n):
@@ -224,20 +221,21 @@
 
 
 def scatter_scratch(shapes, chips):
-    half = (shapes[2][0] // 2, shapes[2][1])
     sem = pltpu.SemaphoreType.DMA
+    across = [(h, w // 2) for h, w in shapes[:2]]
+    down = (shapes[2][0] // 2, shapes[2][1])
     scratch = [pltpu.VMEM((chips, *s), BF) for s in shapes] * 2
-    scratch += [pltpu.VMEM((chips, *s), BF) for s in (shapes[0], half, shapes[1], half)]
-    return scratch + [sem((3, chips))] * 3 + [sem((4, chips - 1))] * 2
+    scratch += [pltpu.VMEM((chips, *s), BF) for s in (across[0], across[0], down, across[1], across[1], down)]
+    return scratch + [sem((3, chips))] * 3 + [sem((6, chips - 1))] * 2
 
 
 def scatter_kernel(chips, *refs):
     grads, done, outs, total = refs[:3], refs[3:6], refs[6:9], refs[9]
-    mine, sq_s, sq_r, pair, pair_sem = refs[25:]
+    mine, sq_s, sq_r, pair, pair_sem = refs[27:]
     z, c, dev = place()
     others = [(z + k) % chips for k in range(1, chips)]
     greet([dev(o, c) for o in others] + [dev(z, 1 - c)])
-    one = Scatter(chips, grads, refs[10:25])
+    one = Scatter(chips, grads, refs[10:27])
     one.start()
     squares = jnp.zeros((), F32)
     for k in range(chips):
@@ -246,9 +244,9 @@
             g = done[k][...].astype(F32)
             outs[k][1] = g
             squares += jnp.sum(g * g)
-    for i, rows, g in one.blocks():
+    for i, rows, cols, g in one.blocks():
         g = g.astype(F32)
-        outs[i][0, rows] = g
+        outs[i][0, rows, cols] = g
         squares += jnp.sum(g * g)
     mine[0] = jnp.full(mine.shape[1:], squares, F32)
     copies = [
@@ -282,8 +280,9 @@
     )(*grads, *done)
 
 
-def blocks(width):
-    return [slice(i, i + COLS) for i in range(0, width, COLS)]
+def blocks(width, cols=None):
+    cols = cols or COLS
+    return [slice(i, i + cols) for i in range(0, width, cols)]
 
 
 def forward_kernel(chips, x_ref, wg, wu, wd, *refs):
@@ -307,7 +306,7 @@
     x = x_ref[0]
     _, _, a = norm_of(x)
     down = jnp.zeros(x.shape, F32)
-    for cols in blocks(wg.shape[1]):
+    for cols in blocks(wg.shape[1], wg.shape[1]):
         gate, up = dot(a, wg[:, cols]), dot(a, wu[:, cols])
         gate_ref[:, cols], up_ref[:, cols] = gate, up
         act = (gate * jax.nn.sigmoid(gate) * up).astype(BF)
@@ -351,7 +350,7 @@
     by_y = dy_ref[0]
     wide, scale, a = norm_of(h_ref[0])
     a_t, by_y_t = a.T, by_y.T
-    by_a_g, by_a_u = jnp.zeros(a.shape, F32), jnp.zeros(a.shape, F32)
+    by_a_g, by_a_u = jnp.zeros(a.shape[::-1], F32), jnp.zeros(a.shape[::-1], F32)
     for cols in blocks(wg.shape[1]):
         gate, up = dot(a, wg[:, cols]), dot(a, wu[:, cols])
         by_act = rounded(dot(by_y, wd[cols, :], 1, 1))
@@ -359,9 +358,9 @@
         ag[:, cols] += dot(a_t, by_gate)
         au[:, cols] += dot(a_t, by_up)
         ad[:, cols] += dot(by_y_t, act)
-        by_a_g += dot(by_gate, wg[:, cols], 1, 1)
-        by_a_u += dot(by_up, wu[:, cols], 1, 1)
-    by_a = rounded(rounded(by_a_g) + rounded(by_a_u))
+        by_a_g += dot(wg[:, cols], by_gate, 1, 1)
+        by_a_u += dot(wu[:, cols], by_up, 1, 1)
+    by_a = (rounded(by_a_g) + rounded(by_a_u)).astype(BF).T.astype(F32)
     by_scale = jnp.sum(by_a * wide, -1, keepdims=True)
     by_h = by_a * scale - wide * (by_scale * scale * scale * scale / wide.shape[-1])
     by_h_ref[0] = (by_y.astype(F32) + rounded(by_h)).astype(BF)
@@ -398,17 +397,17 @@
     @pl.when(t == last)
     def _():
         one.step(chips - 1)
-        for i, rows, g in one.blocks():
-            done[i][rows] = g
+        for i, rows, cols, g in one.blocks():
+            done[i][rows, cols] = g
         one.finish()
 
 
-def tiles(width):
-    return pl.BlockSpec((TILE, width), lambda t: (t, 0))
-
-
-def states(width):
-    return pl.BlockSpec((1, TILE, width), lambda t: (0, t, 0))
+def tiles(width, tile=None):
+    return pl.BlockSpec((tile or TILE, width), lambda t: (t, 0))
+
+
+def states(width, tile=None):
+    return pl.BlockSpec((1, tile or TILE, width), lambda t: (0, t, 0))
 
 
 def whole(shape):
@@ -439,7 +438,8 @@
         grid = tokens // TILE
         flops = 2 * tokens * d * ff
         chips = n // 2
-        assert grid == chips
+        ahead = TILE_FORWARD
+        assert grid == chips and tokens == ahead * len(MOVES)
         wg0, wu0, wd0 = gather_first(weights, n)
         state = jax.ShapeDtypeStruct(x.shape, BF)
         wide = jax.ShapeDtypeStruct((tokens, ff), F32)
@@ -448,8 +448,8 @@
         accs = [pltpu.VMEM(across, F32)] * 3
         ws = [whole(across), whole(across), whole(up_and_down)]
         gate, up, h, *next_w = tiled_call(
-            functools.partial(forward_kernel, chips), grid, [states(d)] + ws + [whole(w.shape) for w in weights],
-            [tiles(ff), tiles(ff), states(d)] + [ANY] * 3, [wide, wide, state] + gathered(weights, n), gather_sems(3, chips), 3 * flops, "forward",
+            functools.partial(forward_kernel, chips), len(MOVES), [states(d, ahead)] + ws + [whole(w.shape) for w in weights],
+            [tiles(ff, ahead), tiles(ff, ahead), states(d, ahead)] + [ANY] * 3, [wide, wide, state] + gathered(weights, n), gather_sems(3, chips), 3 * flops, "forward",
             collective_id=2, has_side_effects=True,
         )(x, wg0, wu0, wd0, *weights)
         by_h, *top = tiled_call(

time: 299 us -> 284 us (0.950)
  Pallas kernels: 291 us -> 276 us
    pallas_call x1, Pallas kernels: 92.9 us -> 87.7 us  [step(): tiled_call(top_kernel, grid, [states(d), states(d)] + ws, [states(d)] + w...]
    pallas_call x1, Pallas kernels: 50 us -> 45.6 us  [scatter_last(): pl.pallas_call(functools.partial(scatter_kernel, chips), out_shape=[jax.S...]
where the time goes in v2:
time: 284 us
  Pallas kernels  276 us (97%)
  other arithmetic  4.92 us (2%)
    pallas_call x1, Pallas kernels, step(): tiled_call(top_kernel, grid, [states(d), states(d)] + ws, [states(d)] + w...  87.7 us
    pallas_call x1, Pallas kernels, step(): tiled_call(functools.partial(bottom_kernel, chips), grid, [states(d), sta...  55.5 us
    pallas_call x1, Pallas kernels, scatter_last(): pl.pallas_call(functools.partial(scatter_kernel, chips), out_shape=[jax.S...  45.6 us
    pallas_call x1, Pallas kernels, step(): tiled_call(functools.partial(forward_kernel, chips), len(MOVES), [states(...  44.9 us
    pallas_call x1, Pallas kernels, gather_first(): pl.pallas_call(functools.partial(gather_kernel, chips), out_shape=gathere...  42.5 us

profile of v2, /device:TPU:21, one launch (start us, length us, event | category | flops | bytes accessed | tf_op | source)
XLA Modules:
  0.0 284.0 jit_solution(14752251617039084368)
XLA Ops:
  0.6 42.5 %gather.1 = (bf16[640,1536]{1,0:T(8,128)(2,1)}, bf16[640,1536]{1,0:T(8,128)(2,1)}, bf16[1536,640]{1,0:T(8,128)(2,1)}) custom-call(bf16[2,40,1536]{2,1,0:T(8,128)(2,1)} %refs_0_.3, bf16[2,40,1536]{2,1,0:T(8,128)(2,1)} %refs_1_.3, bf16[2,96,640]{2,1,0:T(8,128)(2,1)} %refs_2_.3), custom_call_target="tpu_custom_call" | custom-call | tf_op jit(solution)/shard_map/gather/pallas_call | solution.py:135
  43.1 44.9 %forward.1 = (f32[4096,1536]{1,0:T(8,128)}, f32[4096,1536]{1,0:T(8,128)}, bf16[1,4096,640]{2,1,0:T(8,128)(2,1)}, bf16[640,1536]{1,0:T(8,128)(2,1)}, bf16[640,153...) custom-call(bf16[1,4096,640]{2,1,0:T(8,128)(2,1)} %x_ref.3, bf16[640,1536]{1,0:T(8,128)(2,1)} %get-tuple-element.32.wg, ...), custom_call_target="tpu_custom_call" | custom-call | flops 24159191040 | bytes 24159192 | tf_op jit(solution)/shard_map/forward/pallas_call | solution.py:450
  88.1 87.7 %top.1 = (bf16[1,4096,640]{2,1,0:T(8,128)(2,1)}, bf16[640,1536]{1,0:T(8,128)(2,1)}, bf16[640,1536]{1,0:T(8,128)(2,1)}, bf16[1536,640]{1,0:T(8,128)(2,1)}) custom-call(bf16[1,4096,640]{2,1,0:T(8,128)(2,1)} %get-tuple-element.35.h_ref, bf16[1,4096,640]{2,1,0:T(8,128)(2,1)} %dy_ref.1, bf16[640,1536]{1,0:T(8,128)(2,1)} %get-tuple-element.36.wg, ...), custom_call_target="tpu_custom_call" | custom-call | flops 64424509440 | bytes 64424508 | tf_op jit(solution)/shard_map/top/pallas_call | solution.py:455
  175.8 55.5 %bottom.1 = (bf16[640,1536]{1,0:T(8,128)(2,1)}, bf16[640,1536]{1,0:T(8,128)(2,1)}, bf16[1536,640]{1,0:T(8,128)(2,1)}, bf16[40,1536]{1,0:T(8,128)(2,1)}, bf16[40,...) custom-call(bf16[1,4096,640]{2,1,0:T(8,128)(2,1)} %x_ref.3, bf16[1,4096,640]{2,1,0:T(8,128)(2,1)} %get-tuple-element.39.by_y_ref, ...), custom_call_target="tpu_custom_call" | custom-call | flops 32212254720 | bytes 32212254 | tf_op jit(solution)/shard_map/bottom/pallas_call | solution.py:459
  231.2 0.0 copy-start
  231.3 0.0 copy-start.3
  231.3 0.0 copy-start.4
  231.3 45.6 %scatter.1 = (f32[2,40,1536]{2,1,0:T(8,128)}, f32[2,40,1536]{2,1,0:T(8,128)}, f32[2,96,640]{2,1,0:T(8,128)}, f32[8,128]{1,0:T(8,128)}) custom-call(bf16[640,1536]{1,0:T(8,128)(2,1)} %get-tuple-element.45.refs_0_, bf16[640,1536]{1,0:T(8,128)(2,1)} %get-tuple-element.46.refs_1_, bf16[1536,640]{1,0:T(8,128)(2,1)} %get-tuple-element.47.refs_2_, ...), custom_call_target="tpu_custom_call" | custom-call | tf_op jit(solution)/shard_map/scatter/pallas_call | solution.py:272
  276.9 0.0 copy-start.1
  276.9 0.0 copy-start.2
  276.9 0.0 copy-start.5
  276.9 0.0 copy-start.6
  276.9 0.0 copy-start.7
  276.9 0.0 copy-start.8
  277.0 0.0 copy-start.9
  277.0 1.3 slice.3
  279.0 0.0 copy-done
  279.0 0.0 copy-done.3
  279.0 0.0 copy-done.4
  279.0 2.2 fusion.8
  281.2 0.0 copy-done.1
  281.2 0.0 copy-done.2
  281.2 0.0 copy-done.5
  281.2 2.8 fusion.2
  (4 shorter events, 0.0 us)
Async XLA Ops:
  231.2 47.8 %copy-start = (bf16[2,96,640]{2,1,0:T(8,128)(2,1)S(1)}, bf16[2,96,640]{2,1,0:T(8,128)(2,1)}, u32[]{:S(2)}) copy-start(bf16[2,96,640]{2,1,0:T(8,128)(2,1)} %refs_2_.3) | copy-start | bytes 737284
  231.3 47.8 %copy-start.3 = (f32[2,96,640]{2,1,0:T(8,128)S(1)}, f32[2,96,640]{2,1,0:T(8,128)}, u32[]{:S(2)}) copy-start(f32[2,96,640]{2,1,0:T(8,128)} %param.21) | copy-start | bytes 1474564
  231.3 47.8 %copy-start.4 = (f32[2,96,640]{2,1,0:T(8,128)S(1)}, f32[2,96,640]{2,1,0:T(8,128)}, u32[]{:S(2)}) copy-start(f32[2,96,640]{2,1,0:T(8,128)} %param.18) | copy-start | bytes 1474564
  276.9 4.3 %copy-start.1 = (bf16[2,40,1536]{2,1,0:T(8,128)(2,1)S(1)}, bf16[2,40,1536]{2,1,0:T(8,128)(2,1)}, u32[]{:S(2)}) copy-start(bf16[2,40,1536]{2,1,0:T(8,128)(2,1)} %refs_0_.3) | copy-start | bytes 737284
  276.9 4.3 %copy-start.2 = (bf16[2,40,1536]{2,1,0:T(8,128)(2,1)S(1)}, bf16[2,40,1536]{2,1,0:T(8,128)(2,1)}, u32[]{:S(2)}) copy-start(bf16[2,40,1536]{2,1,0:T(8,128)(2,1)} %refs_1_.3) | copy-start | bytes 737284
  276.9 4.3 %copy-start.5 = (f32[2,40,1536]{2,1,0:T(8,128)S(1)}, f32[2,40,1536]{2,1,0:T(8,128)}, u32[]{:S(2)}) copy-start(f32[2,40,1536]{2,1,0:T(8,128)} %param.19) | copy-start | bytes 1474564
  276.9 4.3 %copy-start.6 = (f32[2,40,1536]{2,1,0:T(8,128)S(1)}, f32[2,40,1536]{2,1,0:T(8,128)}, u32[]{:S(2)}) copy-start(f32[2,40,1536]{2,1,0:T(8,128)} %param.16) | copy-start | bytes 1474564
  276.9 4.3 %copy-start.7 = (f32[2,40,1536]{2,1,0:T(8,128)S(1)}, f32[2,40,1536]{2,1,0:T(8,128)}, u32[]{:S(2)}) copy-start(f32[2,40,1536]{2,1,0:T(8,128)} %param.20) | copy-start | bytes 1474564
  276.9 4.3 %copy-start.8 = (f32[2,40,1536]{2,1,0:T(8,128)S(1)}, f32[2,40,1536]{2,1,0:T(8,128)}, u32[]{:S(2)}) copy-start(f32[2,40,1536]{2,1,0:T(8,128)} %param.17) | copy-start | bytes 1474564
  277.0 4.3 %copy-start.9 = (f32[2,40,1536]{2,1,0:T(8,128)S(1)}, f32[2,40,1536]{2,1,0:T(8,128)}, u32[]{:S(2)}) copy-start(f32[2,40,1536]{2,1,0:T(8,128)} %get-tuple-element.51) | copy-start | bytes 1474564

commit v3 on v2

--- a/solution.py
+++ b/solution.py
@@ -15,7 +15,7 @@
 TILE_FORWARD = 256
 COLS = 768
 LIMIT = 60 * 1024 * 1024
-MOVES = (0, 0, 0, 1, 2, 3, 3, 4, 5, 6, 7, 7, 8, 9, 10, 11)
+MOVES = (5, 6, 8, 10, 11, 13, 15, 17, 18, 21, 25, 28, 31)
 
 
 def dot(a, b, ca=1, cb=0):
@@ -108,14 +108,14 @@
     return [pltpu.SemaphoreType.DMA((n, chips - 1))] * 2 + [pltpu.SemaphoreType.DMA((n, chips))] * 2 + [pltpu.SemaphoreType.DMA((n,))]
 
 
-def gathers(chips, layer, shards, outs, sems):
+def gathers(chips, shards, outs, sems):
     z, c, dev = place()
     peers = [dev((z + 1) % chips, c), dev((z + chips - 1) % chips, c), dev(z, 1 - c)]
-    return peers, [Gather(chips, i, reach(i + layer, chips), shards[i].at[layer], outs[i], sems) for i in range(3)]
-
-
-def gather_kernel(chips, *refs):
-    peers, all_of = gathers(chips, 0, refs[:3], refs[3:6], refs[6:])
+    return peers, [Gather(chips, m, reach(m, chips), src, out, sems) for m, (src, out) in enumerate(zip(shards, outs, strict=True))]
+
+
+def gather_kernel(chips, gate, up, *refs):
+    peers, all_of = gathers(chips, (gate.at[0], up.at[0]), refs[:2], refs[2:])
     greet(peers)
     for one in all_of:
         one.start()
@@ -135,9 +135,9 @@
     return pl.pallas_call(
         functools.partial(gather_kernel, chips),
         out_shape=gathered(weights, n),
-        in_specs=[VM] * 3,
-        out_specs=[ANY] * 3,
-        scratch_shapes=gather_sems(3, chips),
+        in_specs=[VM] * 2,
+        out_specs=[ANY] * 2,
+        scratch_shapes=gather_sems(2, chips),
         compiler_params=pltpu.CompilerParams(collective_id=0, has_side_effects=True),
         name="gather",
     )(*weights)
@@ -229,13 +229,13 @@
     return scratch + [sem((3, chips))] * 3 + [sem((6, chips - 1))] * 2
 
 
-def scatter_kernel(chips, *refs):
-    grads, done, outs, total = refs[:3], refs[3:6], refs[6:9], refs[9]
-    mine, sq_s, sq_r, pair, pair_sem = refs[27:]
+def scatter_kernel(chips, count, *refs):
+    grads, done, outs = refs[:3], refs[3:6], refs[6:9]
+    mine, sq_s, sq_r, pair, pair_sem = refs[26:]
     z, c, dev = place()
     others = [(z + k) % chips for k in range(1, chips)]
     greet([dev(o, c) for o in others] + [dev(z, 1 - c)])
-    one = Scatter(chips, grads, refs[10:27])
+    one = Scatter(chips, grads, refs[9:26])
     one.start()
     squares = jnp.zeros((), F32)
     for k in range(chips):
@@ -261,7 +261,10 @@
     copy = pltpu.make_async_remote_copy(src_ref=pair.at[0], dst_ref=pair.at[1], send_sem=pair_sem.at[0], recv_sem=pair_sem.at[1], device_id=dev(z, 1 - c), device_id_type=MESH)
     copy.start()
     copy.wait()
-    total[...] = pair[0] + pair[1]
+    factor = jnp.minimum(1.0, 0.5 * lax.rsqrt((pair[0] + pair[1]) / count + 1e-30))[:1, :1]
+    for out in outs:
+        for l in range(out.shape[0]):
+            out[l] = out[l] * factor
     one.finish()
 
 
@@ -270,10 +273,10 @@
     shapes = block_shapes(grads, n)
     sem = pltpu.SemaphoreType.DMA
     return pl.pallas_call(
-        functools.partial(scatter_kernel, chips),
-        out_shape=[jax.ShapeDtypeStruct((2, *s), F32) for s in shapes] + [jax.ShapeDtypeStruct((8, 128), F32)],
+        functools.partial(scatter_kernel, chips, float(2 * sum(g.size for g in grads))),
+        out_shape=[jax.ShapeDtypeStruct((2, *s), F32) for s in shapes],
         in_specs=[ANY] * 3 + [VM] * 3,
-        out_specs=[VM] * 4,
+        out_specs=[VM] * 3,
         scratch_shapes=scatter_scratch(shapes, chips) + [pltpu.VMEM((chips, 8, 128), F32), sem((chips,)), sem((chips,)), pltpu.VMEM((2, 8, 128), F32), sem((2,))],
         compiler_params=pltpu.CompilerParams(collective_id=1, has_side_effects=True, vmem_limit_bytes=LIMIT),
         name="scatter",
@@ -285,39 +288,53 @@
     return [slice(i, i + cols) for i in range(0, width, cols)]
 
 
-def forward_kernel(chips, x_ref, wg, wu, wd, *refs):
-    shards, (gate_ref, up_ref, h_ref), outs, sems = refs[:3], refs[3:6], refs[6:9], refs[9:]
+def forward_kernel(chips, x_ref, wg, wu, *refs):
+    (gate, up, down), (gate_ref, up_ref, h_ref), outs, act, wd, copied, sems = refs[:3], refs[3:6], refs[6:10], refs[10], refs[11], refs[12], refs[13:]
     t, last = pl.program_id(0), pl.num_programs(0) - 1
-    peers, all_of = gathers(chips, 1, shards, outs, sems)
-    moves = [(one, k) for k in range(1, chips // 2 + 1) for one in all_of]
+    half, tile = pl.num_programs(0) // 2, x_ref.shape[1]
+    peers, all_of = gathers(chips, (down.at[0], gate.at[1], up.at[1], down.at[1]), outs, sems)
+    steps = range(1, chips // 2 + 1)
+    moves = [(one, k) for pair in (all_of[:2], all_of[2:]) for k in steps for one in pair]
 
     @pl.when(t == 0)
     def _():
         greet(peers)
-        for one in all_of:
-            one.start()
-
-    for at, (begin, end) in enumerate(zip(MOVES, MOVES[1:]), 1):
+        all_of[0].start()
+        all_of[1].start()
+
+    for at, (one, k) in zip(MOVES, moves):
         @pl.when(t == at)
         def _():
-            for one, k in moves[begin:end]:
-                one.step(k)
+            one.step(k)
+            if k == len(steps) - 1 and one in all_of[:2]:
+                all_of[2 + all_of.index(one)].start()
 
     x = x_ref[0]
-    _, _, a = norm_of(x)
-    down = jnp.zeros(x.shape, F32)
-    for cols in blocks(wg.shape[1], wg.shape[1]):
-        gate, up = dot(a, wg[:, cols]), dot(a, wu[:, cols])
-        gate_ref[:, cols], up_ref[:, cols] = gate, up
-        act = (gate * jax.nn.sigmoid(gate) * up).astype(BF)
-        down += dot(act, wd[cols, :])
-    h_ref[0] = (x.astype(F32) + rounded(down)).astype(BF)
+
+    @pl.when(t < half)
+    def _():
+        _, _, a = norm_of(x)
+        gate, up = dot(a, wg[...]), dot(a, wu[...])
+        gate_ref[...], up_ref[...] = gate, up
+        act[pl.ds(pl.multiple_of(t * tile, tile), tile)] = (gate * jax.nn.sigmoid(gate) * up).astype(BF)
+
+    @pl.when(t == half)
+    def _():
+        all_of[0].finish()
+        copy = pltpu.make_async_copy(outs[0], wd, copied)
+        copy.start()
+        copy.wait()
+
+    @pl.when(t >= half)
+    def _():
+        down = dot(act[pl.ds(pl.multiple_of((t - half) * tile, tile), tile)], wd[...])
+        h_ref[0] = (x.astype(F32) + rounded(down)).astype(BF)
 
     @pl.when(t == last)
     def _():
-        for one, k in moves[MOVES[-1]:]:
+        for one, k in moves[len(MOVES):]:
             one.step(k)
-        for one in all_of:
+        for one in all_of[1:]:
             one.finish()
 
 
@@ -439,19 +456,24 @@
         flops = 2 * tokens * d * ff
         chips = n // 2
         ahead = TILE_FORWARD
-        assert grid == chips and tokens == ahead * len(MOVES)
-        wg0, wu0, wd0 = gather_first(weights, n)
+        half = tokens // ahead
+        assert grid == chips and MOVES[-1] < 2 * half
+        wg0, wu0 = gather_first(weights[:2], n)
         state = jax.ShapeDtypeStruct(x.shape, BF)
         wide = jax.ShapeDtypeStruct((tokens, ff), F32)
         across, up_and_down = (d, ff), (ff, d)
         grads = [jax.ShapeDtypeStruct(s, BF) for s in (across, across, up_and_down)]
         accs = [pltpu.VMEM(across, F32)] * 3
         ws = [whole(across), whole(across), whole(up_and_down)]
-        gate, up, h, *next_w = tiled_call(
-            functools.partial(forward_kernel, chips), len(MOVES), [states(d, ahead)] + ws + [whole(w.shape) for w in weights],
-            [tiles(ff, ahead), tiles(ff, ahead), states(d, ahead)] + [ANY] * 3, [wide, wide, state] + gathered(weights, n), gather_sems(3, chips), 3 * flops, "forward",
+        ones = pl.BlockSpec((ahead, ff), lambda t: (t - t // half * (t - half + 1), 0))
+        gate, up, h, wd0, *next_w = tiled_call(
+            functools.partial(forward_kernel, chips), 2 * half,
+            [pl.BlockSpec((1, ahead, d), lambda t: (0, t % half, 0)), ws[0], ws[1]] + [whole(w.shape) for w in weights],
+            [ones, ones, pl.BlockSpec((1, ahead, d), lambda t: (0, t // half * (t - half), 0))] + [ANY] * 4,
+            [wide, wide, state] + gathered((weights[2], *weights), n),
+            [pltpu.VMEM((tokens, ff), BF), pltpu.VMEM(up_and_down, BF), pltpu.SemaphoreType.DMA(())] + gather_sems(4, chips), 3 * flops, "forward",
             collective_id=2, has_side_effects=True,
-        )(x, wg0, wu0, wd0, *weights)
+        )(x, wg0, wu0, *weights)
         by_h, *top = tiled_call(
             top_kernel, grid, [states(d), states(d)] + ws, [states(d)] + ws, [state] + grads, accs, 8 * flops, "top"
         )(h, dy, *next_w)
@@ -461,10 +483,8 @@
             ws + [whole(b) for b in shapes], grads + [jax.ShapeDtypeStruct(b, BF) for b in shapes],
             accs + scatter_scratch(shapes, chips), 4 * flops, "bottom", collective_id=3, has_side_effects=True,
         )(x, by_h, gate, up, wd0, *top)
-        *mine, squares = scatter_last(bottom, (b0, b1, b2), n)
-        count = n * sum(g.size for g in mine)
-        factor = jnp.minimum(1.0, 0.5 * lax.rsqrt(squares[0, 0] / count + 1e-30))
-        new = [adamw(w.astype(F32), m, v, g * factor) for w, m, v, g in zip(weights, m, v, mine, strict=True)]
+        mine = scatter_last(bottom, (b0, b1, b2), n)
+        new = [adamw(w.astype(F32), m, v, g) for w, m, v, g in zip(weights, m, v, mine, strict=True)]
         return tuple(one[which] for which in range(3) for one in new)
 
     states_spec, cut = P(("rep", "dp"), None, None), P(None, "dp", None)

time: 284 us -> 292 us (1.028)
  Pallas kernels: 276 us -> 286 us
    pallas_call x2, Pallas kernels: 90.5 us -> 108 us  [the longest x1 61.7 us: step(): tiled_call(functools.partial(forward_kernel, chips), 2 * half, [pl.BlockS...]
    pallas_call x1, Pallas kernels: 42.5 us -> 34.4 us  [gather_first(): pl.pallas_call(functools.partial(gather_kernel, chips), out_shape=gathere...]
where the time goes in v3:
time: 292 us
  Pallas kernels  286 us (98%)
  other arithmetic  5.03 us (2%)
    pallas_call x1, Pallas kernels, step(): tiled_call(top_kernel, grid, [states(d), states(d)] + ws, [states(d)] + w...  87.7 us
    pallas_call x1, Pallas kernels, step(): tiled_call(functools.partial(forward_kernel, chips), 2 * half, [pl.BlockS...  61.7 us
    pallas_call x1, Pallas kernels, step(): tiled_call(functools.partial(bottom_kernel, chips), grid, [states(d), sta...  56 us
    pallas_call x1, Pallas kernels, scatter_last(): pl.pallas_call(functools.partial(scatter_kernel, chips, float(2 * sum((g....  45.8 us
    pallas_call x1, Pallas kernels, gather_first(): pl.pallas_call(functools.partial(gather_kernel, chips), out_shape=gathere...  34.4 us

profile of v3, /device:TPU:21, one launch (start us, length us, event | category | flops | bytes accessed | tf_op | source)
XLA Modules:
  0.0 291.5 jit_solution(3678924616658564099)
XLA Ops:
  0.6 34.4 %gather.1 = (bf16[640,1536]{1,0:T(8,128)(2,1)}, bf16[640,1536]{1,0:T(8,128)(2,1)}) custom-call(bf16[2,40,1536]{2,1,0:T(8,128)(2,1)} %refs_0_.1, bf16[2,40,1536]{2,1,0:T(8,128)(2,1)} %refs_1_.1), custom_call_target="tpu_custom_call" | custom-call | tf_op jit(solution)/shard_map/gather/pallas_call | solution.py:135
  35.1 61.7 %forward.1 = (f32[4096,1536]{1,0:T(8,128)}, f32[4096,1536]{1,0:T(8,128)}, bf16[1,4096,640]{2,1,0:T(8,128)(2,1)}, bf16[1536,640]{1,0:T(8,128)(2,1)}, bf16[640,153...) custom-call(bf16[1,4096,640]{2,1,0:T(8,128)(2,1)} %x_ref.3, ...), custom_call_target="tpu_custom_call" | custom-call | flops 24159191040 | bytes 24159192 | tf_op jit(solution)/shard_map/forward/pallas_call | solution.py:469
  96.8 87.7 %top.1 = (bf16[1,4096,640]{2,1,0:T(8,128)(2,1)}, bf16[640,1536]{1,0:T(8,128)(2,1)}, bf16[640,1536]{1,0:T(8,128)(2,1)}, bf16[1536,640]{1,0:T(8,128)(2,1)}) custom-call(bf16[1,4096,640]{2,1,0:T(8,128)(2,1)} %get-tuple-element.33.h_ref, bf16[1,4096,640]{2,1,0:T(8,128)(2,1)} %dy_ref.1, bf16[640,1536]{1,0:T(8,128)(2,1)} %get-tuple-element.34.wg, ...), custom_call_target="tpu_custom_call" | custom-call | flops 64424509440 | bytes 64424508 | tf_op jit(solution)/shard_map/top/pallas_call | solution.py:477
  184.5 56.0 %bottom.1 = (bf16[640,1536]{1,0:T(8,128)(2,1)}, bf16[640,1536]{1,0:T(8,128)(2,1)}, bf16[1536,640]{1,0:T(8,128)(2,1)}, bf16[40,1536]{1,0:T(8,128)(2,1)}, bf16[40,...) custom-call(bf16[1,4096,640]{2,1,0:T(8,128)(2,1)} %x_ref.3, bf16[1,4096,640]{2,1,0:T(8,128)(2,1)} %get-tuple-element.37.by_y_ref, ...), custom_call_target="tpu_custom_call" | custom-call | flops 32212254720 | bytes 32212254 | tf_op jit(solution)/shard_map/bottom/pallas_call | solution.py:481
  240.5 0.0 copy-start.2
  240.5 0.0 copy-start.3
  240.5 0.0 copy-start.9
  240.5 45.8 %scatter.1 = (f32[2,40,1536]{2,1,0:T(8,128)}, f32[2,40,1536]{2,1,0:T(8,128)}, f32[2,96,640]{2,1,0:T(8,128)}) custom-call(bf16[640,1536]{1,0:T(8,128)(2,1)} %get-tuple-element.44.refs_0_, bf16[640,1536]{1,0:T(8,128)(2,1)} %get-tuple-element.45.refs_1_, bf16[1536,640]{1,0:T(8,128)(2,1)} %get-tuple-element.46.refs_2_, ...), custom_call_target="tpu_custom_call" | custom-call | tf_op jit(solution)/shard_map/scatter/pallas_call | solution.py:275
  286.3 0.0 copy-start
  286.3 0.0 copy-start.1
  286.4 0.0 copy-start.4
  286.4 0.0 copy-start.5
  286.4 0.0 copy-start.6
  286.4 0.0 copy-start.7
  286.4 0.0 copy-start.8
  286.4 0.0 copy-done.2
  286.4 0.0 copy-done.3
  286.4 0.0 copy-done.9
  286.4 2.3 fusion.8
  288.8 0.0 copy-done
  288.8 0.0 copy-done.1
  288.8 0.0 copy-done.4
  288.8 0.0 copy-done.5
  288.8 2.7 fusion.2
  (3 shorter events, 0.0 us)
Async XLA Ops:
  240.5 45.9 %copy-start.2 = (f32[2,96,640]{2,1,0:T(8,128)S(1)}, f32[2,96,640]{2,1,0:T(8,128)}, u32[]{:S(2)}) copy-start(f32[2,96,640]{2,1,0:T(8,128)} %param.21) | copy-start | bytes 1474564
  240.5 45.9 %copy-start.3 = (f32[2,96,640]{2,1,0:T(8,128)S(1)}, f32[2,96,640]{2,1,0:T(8,128)}, u32[]{:S(2)}) copy-start(f32[2,96,640]{2,1,0:T(8,128)} %param.18) | copy-start | bytes 1474564
  240.5 45.9 %copy-start.9 = (bf16[2,96,640]{2,1,0:T(8,128)(2,1)S(1)}, bf16[2,96,640]{2,1,0:T(8,128)(2,1)}, u32[]{:S(2)}) copy-start(bf16[2,96,640]{2,1,0:T(8,128)(2,1)} %refs_2_.1) | copy-start | bytes 737284
  286.3 2.4 copy-start
  286.3 2.4 copy-start.1
  286.4 2.4 copy-start.4
  286.4 2.4 copy-start.5
  286.4 2.4 copy-start.6
  286.4 2.4 copy-start.7
  286.4 2.4 copy-start.8

commit v4 on v2

--- a/solution.py
+++ b/solution.py
@@ -229,13 +229,13 @@
     return scratch + [sem((3, chips))] * 3 + [sem((6, chips - 1))] * 2
 
 
-def scatter_kernel(chips, *refs):
-    grads, done, outs, total = refs[:3], refs[3:6], refs[6:9], refs[9]
-    mine, sq_s, sq_r, pair, pair_sem = refs[27:]
+def scatter_kernel(chips, count, *refs):
+    grads, done, outs = refs[:3], refs[3:6], refs[6:9]
+    mine, sq_s, sq_r, pair, pair_sem = refs[26:]
     z, c, dev = place()
     others = [(z + k) % chips for k in range(1, chips)]
     greet([dev(o, c) for o in others] + [dev(z, 1 - c)])
-    one = Scatter(chips, grads, refs[10:27])
+    one = Scatter(chips, grads, refs[9:26])
     one.start()
     squares = jnp.zeros((), F32)
     for k in range(chips):
@@ -261,7 +261,10 @@
     copy = pltpu.make_async_remote_copy(src_ref=pair.at[0], dst_ref=pair.at[1], send_sem=pair_sem.at[0], recv_sem=pair_sem.at[1], device_id=dev(z, 1 - c), device_id_type=MESH)
     copy.start()
     copy.wait()
-    total[...] = pair[0] + pair[1]
+    factor = jnp.minimum(1.0, 0.5 * lax.rsqrt((pair[0] + pair[1]) / count + 1e-30))[:1, :1]
+    for out in outs:
+        for l in range(out.shape[0]):
+            out[l] = out[l] * factor
     one.finish()
 
 
@@ -270,10 +273,10 @@
     shapes = block_shapes(grads, n)
     sem = pltpu.SemaphoreType.DMA
     return pl.pallas_call(
-        functools.partial(scatter_kernel, chips),
-        out_shape=[jax.ShapeDtypeStruct((2, *s), F32) for s in shapes] + [jax.ShapeDtypeStruct((8, 128), F32)],
+        functools.partial(scatter_kernel, chips, float(2 * sum(g.size for g in grads))),
+        out_shape=[jax.ShapeDtypeStruct((2, *s), F32) for s in shapes],
         in_specs=[ANY] * 3 + [VM] * 3,
-        out_specs=[VM] * 4,
+        out_specs=[VM] * 3,
         scratch_shapes=scatter_scratch(shapes, chips) + [pltpu.VMEM((chips, 8, 128), F32), sem((chips,)), sem((chips,)), pltpu.VMEM((2, 8, 128), F32), sem((2,))],
         compiler_params=pltpu.CompilerParams(collective_id=1, has_side_effects=True, vmem_limit_bytes=LIMIT),
         name="scatter",
@@ -461,10 +464,8 @@
             ws + [whole(b) for b in shapes], grads + [jax.ShapeDtypeStruct(b, BF) for b in shapes],
             accs + scatter_scratch(shapes, chips), 4 * flops, "bottom", collective_id=3, has_side_effects=True,
         )(x, by_h, gate, up, wd0, *top)
-        *mine, squares = scatter_last(bottom, (b0, b1, b2), n)
-        count = n * sum(g.size for g in mine)
-        factor = jnp.minimum(1.0, 0.5 * lax.rsqrt(squares[0, 0] / count + 1e-30))
-        new = [adamw(w.astype(F32), m, v, g * factor) for w, m, v, g in zip(weights, m, v, mine, strict=True)]
+        mine = scatter_last(bottom, (b0, b1, b2), n)
+        new = [adamw(w.astype(F32), m, v, g) for w, m, v, g in zip(weights, m, v, mine, strict=True)]
         return tuple(one[which] for which in range(3) for one in new)
 
     states_spec, cut = P(("rep", "dp"), None, None), P(None, "dp", None)

time: 284 us -> 282 us (level)
  no operation moved by 1% of the time
where the time goes in v4:
time: 282 us
  Pallas kernels  276 us (98%)
  other arithmetic  5.03 us (2%)
    pallas_call x1, Pallas kernels, step(): tiled_call(top_kernel, grid, [states(d), states(d)] + ws, [states(d)] + w...  87.7 us
    pallas_call x1, Pallas kernels, step(): tiled_call(functools.partial(bottom_kernel, chips), grid, [states(d), sta...  55.5 us
    pallas_call x1, Pallas kernels, scatter_last(): pl.pallas_call(functools.partial(scatter_kernel, chips, float(2 * sum((g....  45.7 us
    pallas_call x1, Pallas kernels, step(): tiled_call(functools.partial(forward_kernel, chips), len(MOVES), [states(...  44.9 us
    pallas_call x1, Pallas kernels, gather_first(): pl.pallas_call(functools.partial(gather_kernel, chips), out_shape=gathere...  42.5 us

profile of v4, /device:TPU:21, one launch (start us, length us, event | category | flops | bytes accessed | tf_op | source)
XLA Modules:
  0.0 282.2 jit_solution(1062230210960365283)
XLA Ops:
  0.6 42.5 %gather.1 = (bf16[640,1536]{1,0:T(8,128)(2,1)}, bf16[640,1536]{1,0:T(8,128)(2,1)}, bf16[1536,640]{1,0:T(8,128)(2,1)}) custom-call(bf16[2,40,1536]{2,1,0:T(8,128)(2,1)} %refs_0_.3, bf16[2,40,1536]{2,1,0:T(8,128)(2,1)} %refs_1_.3, bf16[2,96,640]{2,1,0:T(8,128)(2,1)} %refs_2_.3), custom_call_target="tpu_custom_call" | custom-call | tf_op jit(solution)/shard_map/gather/pallas_call | solution.py:135
  43.1 44.9 %forward.1 = (f32[4096,1536]{1,0:T(8,128)}, f32[4096,1536]{1,0:T(8,128)}, bf16[1,4096,640]{2,1,0:T(8,128)(2,1)}, bf16[640,1536]{1,0:T(8,128)(2,1)}, bf16[640,153...) custom-call(bf16[1,4096,640]{2,1,0:T(8,128)(2,1)} %x_ref.3, bf16[640,1536]{1,0:T(8,128)(2,1)} %get-tuple-element.31.wg, ...), custom_call_target="tpu_custom_call" | custom-call | flops 24159191040 | bytes 24159192 | tf_op jit(solution)/shard_map/forward/pallas_call | solution.py:453
  88.0 87.7 %top.1 = (bf16[1,4096,640]{2,1,0:T(8,128)(2,1)}, bf16[640,1536]{1,0:T(8,128)(2,1)}, bf16[640,1536]{1,0:T(8,128)(2,1)}, bf16[1536,640]{1,0:T(8,128)(2,1)}) custom-call(bf16[1,4096,640]{2,1,0:T(8,128)(2,1)} %get-tuple-element.34.h_ref, bf16[1,4096,640]{2,1,0:T(8,128)(2,1)} %dy_ref.1, bf16[640,1536]{1,0:T(8,128)(2,1)} %get-tuple-element.35.wg, ...), custom_call_target="tpu_custom_call" | custom-call | flops 64424509440 | bytes 64424508 | tf_op jit(solution)/shard_map/top/pallas_call | solution.py:458
  175.8 55.5 %bottom.1 = (bf16[640,1536]{1,0:T(8,128)(2,1)}, bf16[640,1536]{1,0:T(8,128)(2,1)}, bf16[1536,640]{1,0:T(8,128)(2,1)}, bf16[40,1536]{1,0:T(8,128)(2,1)}, bf16[40,...) custom-call(bf16[1,4096,640]{2,1,0:T(8,128)(2,1)} %x_ref.3, bf16[1,4096,640]{2,1,0:T(8,128)(2,1)} %get-tuple-element.38.by_y_ref, ...), custom_call_target="tpu_custom_call" | custom-call | flops 32212254720 | bytes 32212254 | tf_op jit(solution)/shard_map/bottom/pallas_call | solution.py:462
  231.2 0.0 copy-start
  231.3 0.0 copy-start.3
  231.3 0.0 copy-start.4
  231.3 45.7 %scatter.1 = (f32[2,40,1536]{2,1,0:T(8,128)}, f32[2,40,1536]{2,1,0:T(8,128)}, f32[2,96,640]{2,1,0:T(8,128)}) custom-call(bf16[640,1536]{1,0:T(8,128)(2,1)} %get-tuple-element.44.refs_0_, bf16[640,1536]{1,0:T(8,128)(2,1)} %get-tuple-element.45.refs_1_, bf16[1536,640]{1,0:T(8,128)(2,1)} %get-tuple-element.46.refs_2_, ...), custom_call_target="tpu_custom_call" | custom-call | tf_op jit(solution)/shard_map/scatter/pallas_call | solution.py:275
  277.0 0.0 copy-start.1
  277.0 0.0 copy-start.2
  277.0 0.0 copy-start.5
  277.1 0.0 copy-start.6
  277.1 0.0 copy-start.7
  277.1 0.0 copy-start.8
  277.1 0.0 copy-start.9
  277.1 0.0 copy-done
  277.1 0.0 copy-done.3
  277.1 0.0 copy-done.4
  277.1 2.3 fusion.8
  279.4 0.0 copy-done.1
  279.4 0.0 copy-done.2
  279.4 0.0 copy-done.5
  279.5 0.0 copy-done.6
  279.5 2.7 fusion.2
  (3 shorter events, 0.0 us)
Async XLA Ops:
  231.2 45.9 %copy-start = (bf16[2,96,640]{2,1,0:T(8,128)(2,1)S(1)}, bf16[2,96,640]{2,1,0:T(8,128)(2,1)}, u32[]{:S(2)}) copy-start(bf16[2,96,640]{2,1,0:T(8,128)(2,1)} %refs_2_.3) | copy-start | bytes 737284
  231.3 45.9 %copy-start.3 = (f32[2,96,640]{2,1,0:T(8,128)S(1)}, f32[2,96,640]{2,1,0:T(8,128)}, u32[]{:S(2)}) copy-start(f32[2,96,640]{2,1,0:T(8,128)} %param.21) | copy-start | bytes 1474564
  231.3 45.9 %copy-start.4 = (f32[2,96,640]{2,1,0:T(8,128)S(1)}, f32[2,96,640]{2,1,0:T(8,128)}, u32[]{:S(2)}) copy-start(f32[2,96,640]{2,1,0:T(8,128)} %param.18) | copy-start | bytes 1474564
  277.0 2.4 copy-start.1
  277.0 2.4 copy-start.2
  277.0 2.4 copy-start.5
  277.1 2.4 copy-start.6
  277.1 2.4 copy-start.7
  277.1 2.4 copy-start.8
  277.1 2.4 copy-start.9
